TPU v7x, 32 devices: a whole 2x2x4 slice. The times are simulated.
32 devices in a mesh: band: 8 (over z, core), lane: 4 (over y, x).
Axes of the slice: x: 2, y: 2, z: 4, core: 2. Of those that a mesh axis runs over, the one named last changes fastest.
Arguments:
- first_factor: bfloat16 [8192, 4096], P('band', 'lane'), may hold values from -6 to 6
- second_factor: bfloat16 [4096, 2048], P('band', 'lane'), may hold values from -0.09375 to 0.09375
- result_in: float32 [8192, 2048], P('band', 'lane'), may hold values from -6 to 6
- pivot_scale: float32 [4096], replicated, may hold values from 0.25 to 1.75
Outputs:
- updated: float32 [8192, 2048], P('band', 'lane')
All inputs are finite; a program needn't handle non-finite values.
Results may differ from a plain program's by a relative error of at most 0.002.
Values may be sent and summed in bfloat16 or wider, within the bound.
No kernel may reach another device: no remote copies, remote signals or barrier semaphores. Data moves between devices by JAX's collectives and lax.ppermute only.
A program may use at most 128 MiB of HBM per device.

v0:
```python
import jax
import jax.numpy as jnp
from jax import lax
from jax.sharding import PartitionSpec as P


def join_panel(left_panel, right_panel):
    return jnp.dot(left_panel, right_panel, preferred_element_type=jnp.float32)


def on_device(first_factor, second_factor, result_in, pivot_scale):
    share = first_factor.shape[1]
    part_scale = lax.dynamic_slice_in_dim(pivot_scale, lax.axis_index("lane") * share, share)
    scaled_left = (first_factor.astype(jnp.float32) * part_scale).astype(jnp.bfloat16)
    left_line = lax.all_gather(scaled_left, "lane", axis=1, tiled=True)
    total = join_panel(left_line, lax.all_gather(second_factor, "band", axis=0, tiled=True))
    updated = result_in - total
    row_power = lax.psum(jnp.sum(updated * updated, axis=1), "lane")
    updated = (
        updated * lax.rsqrt(row_power / (updated.shape[1] * lax.axis_size("lane")) + 1e-06)[:, None]
    )
    return updated


def solution(mesh):
    return jax.shard_map(
        on_device,
        mesh=mesh,
        in_specs=(P("band", "lane"), P("band", "lane"), P("band", "lane"), P()),
        out_specs=P("band", "lane"),
        check_vma=False,
    )
```

profile of v0, /device:TPU:0, one launch (start us, length us, event | category | flops | bytes accessed | tf_op | source)
XLA Modules:
  0.0 177.2 jit_solution(5245780658395474004)
XLA Ops:
  6.5 0.0 all-gather.5.cloned.1.call-start
  6.5 0.7 all-gather.5.cloned.1.call-update
  7.3 0.0 all-gather.3.cloned.1.call-start
  7.3 0.7 dynamic_slice.3
  8.0 3.5 %multiply_convert_fusion = bf16[1024,1024]{1,0:T(8,128)(2,1)} fusion(bf16[1024,1024]{1,0:T(8,128)(2,1)} %param.4, f32[1024]{0:T(1024)S(1)} %dynamic_slice.3), kind=kLoop, calls=%fused_computation | loop fusion | flops 3145728 | bytes 4198400 | tf_op jit(solution)/shard_map/convert_element_type | solution.py:14
  11.5 0.0 copy-start
  11.5 0.0 all-gather.3.cloned.1.call-update
  11.5 1.6 copy-done
  13.1 1.8 %copy.5 = f32[1024,512]{0,1:T(8,128)} copy(f32[1024,512]{1,0:T(8,128)S(1)} %copy-done) | data formatting | bytes 4194304 | tf_op args[2]
  14.9 43.7 %all-gather.5.cloned.1.call-done = bf16[4096,512]{1,0:T(8,128)(2,1)} async-done(((bf16[512,512]{1,0:T(8,128)(2,1)}), bf16[4096,512]{1,0:T(8,128)(2,1)}) %all-gather.5.cloned.1.call-update) | async-done | bytes 4194320 | tf_op jit(solution)/shard_map/all_gather | solution.py:16
  58.6 88.2 %all-gather.3.cloned.1.call-done = bf16[1024,4096]{1,0:T(8,128)(2,1)} async-done(((bf16[1024,1024]{1,0:T(8,128)(2,1)}), bf16[1024,4096]{1,0:T(8,128)(2,1)}) %all-gather.3.cloned.1.call-update) | async-done | bytes 8388624 | tf_op jit(solution)/shard_map/all_gather | solution.py:15
  146.7 11.1 %multiply_reduce_fusion = (f32[1024]{0:T(1024)S(1)}, f32[1024,512]{0,1:T(8,128)}) fusion(f32[1024,512]{0,1:T(8,128)} %copy.5, bf16[1024,4096]{1,0:T(8,128)(2,1)} %all-gather.3.cloned.1.call-done, bf16[4096,512]{1,0:T(8,128)(2,1)} %all-gather.5.cloned.1.call-done), kind=kOutput, calls=%fused_computation.1 | convolution fusion | flops 4296539136 | bytes 16781312 | tf_op jit(solution)/shard_map/dot_general | solution.py:8
  157.8 8.9 %psum.7 = f32[1024]{0:T(1024)S(1)} all-reduce(f32[1024]{0:T(1024)S(1)} %get-tuple-element.5), channel_id=1, replica_groups=mesh['band'=8,'lane'=4] {'lane'}, use_global_device_ids=true, to_apply=%region_1.0 | all-reduce | flops 1024 | bytes 8192 | tf_op jit(solution)/shard_map/psum | solution.py:18
  166.7 1.8 %broadcast_multiply_fusion = f32[1024,512]{0,1:T(8,128)S(1)} fusion(f32[1024,512]{0,1:T(8,128)} %get-tuple-element.6, f32[1024]{0:T(1024)S(1)} %add_rsqrt_fusion), kind=kLoop, calls=%fused_computation.3 | loop fusion | flops 524288 | bytes 4198400 | tf_op jit(solution)/shard_map/mul | solution.py:20
  168.6 1.8 %copy.6 = f32[1024,512]{1,0:T(8,128)} copy(f32[1024,512]{0,1:T(8,128)S(1)} %broadcast_multiply_fusion) | data formatting | bytes 4194304 | tf_op jit(solution)/shard_map/mul | solution.py:20
  (1 shorter events, 0.0 us)
Async XLA Ops:
  6.5 52.0 %all-gather.5.cloned.1.call-start = ((), (), s32[]{:S(2)}) async-start(), calls=%async_computation.1 | async-start | bytes 4718592 | tf_op jit(solution)/shard_map/all_gather | solution.py:16
  7.3 139.5 %all-gather.3.cloned.1.call-start = ((), (), s32[]{:S(2)}) async-start(), calls=%async_computation | async-start | bytes 10485760 | tf_op jit(solution)/shard_map/all_gather | solution.py:15
  11.5 1.6 copy-start
Sparse Core Ops, SparseCore 0:
  8.9 49.5 all-gather.4
  60.4 86.2 all-gather.2
where the time goes:
time: 177 us
  waiting for transfers between devices  133 us (75%)
  between operations  13.4 us (8%)
  matrix products  11.1 us (6%)
  blocking collectives  8.9 us (5%)
  local copies, waits for them, and re-layouts  5.88 us (3%)
  other arithmetic  5.32 us (3%)
    all_gather x1, waiting for transfers between devices, on_device(): left_line = lax.all_gather(scaled_left, 'lane', axis=1, tiled=True)  88.2 us
    all_gather x1, waiting for transfers between devices, on_device(): lax.all_gather(second_factor, 'band', axis=0, tiled=True)  43.7 us
    dot_general x1, matrix products, join_panel(): return jnp.dot(left_panel, right_panel, preferred_element_type=jnp.float32)  11.1 us
    psum x1, blocking collectives, on_device(): row_power = lax.psum(jnp.sum(updated * updated, axis=1), 'lane')  8.9 us
  transfers between devices with their start and end apart: 2, of which 2 were waited for; matrix products, arithmetic and copies ran while one was open for 3% of the time, Pallas kernels for 0%

commit v1 on v0

v1 whole, which is shorter than its diff:
```python
import functools

import jax
import jax.numpy as jnp
from jax import lax
from jax.experimental import pallas as pl
from jax.experimental.pallas import tpu as pltpu
from jax.sharding import PartitionSpec as P


CORES = 2
EPS = 1e-06
LANES = 128
VMEM_LIMIT = 60 * 1024 * 1024


def cost(flops, nbytes):
    return pl.CostEstimate(flops=int(flops), bytes_accessed=int(nbytes), transcendentals=0)


def vmem():
    return pl.BlockSpec(memory_space=pltpu.VMEM)


def params():
    return pltpu.CompilerParams(vmem_limit_bytes=VMEM_LIMIT)


def scale_kernel(lane_ref, left_ref, scale_ref, *outs):
    scale = scale_ref[...].reshape(1, -1)
    height = outs[0].shape[0]
    for at, out in enumerate(outs):
        rows = left_ref[at * height:(at + 1) * height, :]
        out[...] = (rows.astype(jnp.float32) * scale).astype(jnp.bfloat16)


def scaled_pieces(lane, left, scale, block, blocks, count):
    rows, depth = left.shape
    height = rows // blocks
    piece = jax.ShapeDtypeStruct((height // count, depth), jnp.bfloat16)
    return pl.pallas_call(
        scale_kernel,
        grid_spec=pltpu.PrefetchScalarGridSpec(
            num_scalar_prefetch=1,
            grid=(1,),
            in_specs=[
                pl.BlockSpec((height, depth), lambda i, lane: (block, 0)),
                pl.BlockSpec((depth,), lambda i, lane: (lane[0],)),
            ],
            out_specs=[pl.BlockSpec(piece.shape, lambda i, lane: (0, 0))] * count,
        ),
        out_shape=[piece] * count,
        cost_estimate=cost(2 * height * depth, 4 * height * depth),
        compiler_params=params(),
    )(lane, left, scale)


def lay_kernel(chips, where_ref, *refs):
    mine, other, out, sems = refs[:chips], refs[chips:2 * chips], refs[-2], refs[-1]
    depth = mine[0].shape[0]
    z, core = where_ref[0], where_ref[1]
    copies = []
    for step in range(chips):
        base = lax.rem(z - step + chips, chips) * (CORES * depth)
        for at, (source, half) in enumerate(((mine[step], core), (other[step], 1 - core))):
            start = pl.multiple_of(base + half * depth, depth)
            copies.append(
                pltpu.make_async_copy(source, out.at[pl.ds(start, depth), :], sems.at[step, at])
            )
    for copy in copies:
        copy.start()
    for copy in copies:
        copy.wait()


def laid(where, mine, other):
    chips = len(mine)
    depth, width = mine[0].shape
    total = chips * CORES * depth
    return pl.pallas_call(
        functools.partial(lay_kernel, chips),
        in_specs=[pl.BlockSpec(memory_space=pltpu.SMEM)]
        + [pl.BlockSpec(memory_space=pl.ANY)] * (2 * chips),
        out_specs=vmem(),
        out_shape=jax.ShapeDtypeStruct((total, width), jnp.bfloat16),
        scratch_shapes=[pltpu.SemaphoreType.DMA((chips, CORES))],
        cost_estimate=cost(total * width, 4 * total * width),
        compiler_params=params(),
    )(where, *mine, *other)


def product_kernel(plan, squares, where_ref, right_ref, *refs):
    n_rows = len(plan)
    n_left = 1 + max(at for terms in plan for at, _ in terms)
    bases, lefts = refs[:n_rows], refs[n_rows:n_rows + n_left]
    outs = refs[n_rows + n_left + squares:n_rows + n_left + squares + n_rows]
    lane = where_ref[2]
    depth = lefts[0].shape[1]
    for at, terms in enumerate(plan):
        total = bases[at][...]
        for left, distance in terms:
            part = lax.bitwise_xor(lane, distance)
            start = pl.multiple_of(part * depth, depth)
            total = total - jnp.dot(
                lefts[left][...], right_ref[pl.ds(start, depth), :],
                preferred_element_type=jnp.float32,
            )
        outs[at][...] = total


def power_rows(block):
    squares = block * block
    folded = squares[:, :LANES]
    for at in range(1, block.shape[1] // LANES):
        folded = folded + squares[:, at * LANES:(at + 1) * LANES]
    return jnp.sum(folded.T, axis=0, keepdims=True)


def products(where, right, bases, lefts, plan):
    flops = sum(2 * lefts[at].shape[0] * lefts[at].shape[1] * right.shape[1] for terms in plan for at, _ in terms)
    return pl.pallas_call(
        functools.partial(product_kernel, plan, 0),
        in_specs=[pl.BlockSpec(memory_space=pltpu.SMEM)] + [vmem()] * (1 + len(bases) + len(lefts)),
        out_specs=[vmem()] * len(bases),
        out_shape=[jax.ShapeDtypeStruct(base.shape, jnp.float32) for base in bases],
        cost_estimate=cost(flops, flops / 512),
        compiler_params=params(),
    )(where, right, *bases, *lefts)


def first_kernel(plan, where_ref, right_ref, base_ref, *refs):
    height = refs[0].shape[0]
    bases = [base_ref.at[at * height:(at + 1) * height, :] for at in range(len(plan))]
    product_kernel(plan, 0, where_ref, right_ref, *bases, *refs)


def first_products(where, right, base, lefts, plan):
    height = lefts[0].shape[0]
    flops = sum(2 * height * lefts[at].shape[1] * right.shape[1] for terms in plan for at, _ in terms)
    return pl.pallas_call(
        functools.partial(first_kernel, plan),
        in_specs=[pl.BlockSpec(memory_space=pltpu.SMEM)] + [vmem()] * (2 + len(lefts)),
        out_specs=[vmem()] * len(plan),
        out_shape=[jax.ShapeDtypeStruct((height, base.shape[1]), jnp.float32)] * len(plan),
        cost_estimate=cost(flops, flops / 512),
        compiler_params=params(),
    )(where, right, base, *lefts)


def last_kernel(plan, n_done, where_ref, right_ref, *refs):
    n_rows = len(plan)
    n_left = 1 + max(at for terms in plan for at, _ in terms)
    done, rest = refs[:n_done], refs[n_done:]
    power_ref = rest[-1]
    product_kernel(plan, 0, where_ref, right_ref, *rest[:-1])
    outs = rest[n_rows + n_left:-1]
    at = 0
    for ref in (*done, *outs):
        for block in range(ref.shape[0] // LANES):
            power_ref[at:at + 1, :] = power_rows(ref[block * LANES:(block + 1) * LANES, :])
            at += 1


def last_products(where, right, done, bases, lefts, plan):
    flops = sum(2 * lefts[at].shape[0] * lefts[at].shape[1] * right.shape[1] for terms in plan for at, _ in terms)
    rows = sum(a.shape[0] for a in (*done, *bases))
    *outs, power = pl.pallas_call(
        functools.partial(last_kernel, plan, len(done)),
        in_specs=[pl.BlockSpec(memory_space=pltpu.SMEM)]
        + [vmem()] * (1 + len(done) + len(bases) + len(lefts)),
        out_specs=[vmem()] * (len(bases) + 1),
        out_shape=[jax.ShapeDtypeStruct(base.shape, jnp.float32) for base in bases]
        + [jax.ShapeDtypeStruct((rows // LANES, LANES), jnp.float32)],
        cost_estimate=cost(flops, flops / 512),
        compiler_params=params(),
    )(where, right, *done, *bases, *lefts)
    return outs, power


def norm_kernel(columns, n_power, *refs):
    powers, blocks, out = refs[:n_power], refs[n_power:-1], refs[-1]
    power = powers[0][...]
    for ref in powers[1:]:
        power = power + ref[...]
    factor = lax.rsqrt(power / columns + EPS)
    at = 0
    for ref in blocks:
        for block in range(ref.shape[0] // LANES):
            spread = jnp.broadcast_to(factor[at:at + 1, :], (LANES, LANES)).T
            for tile in range(ref.shape[1] // LANES):
                columns_at = slice(tile * LANES, (tile + 1) * LANES)
                out[at * LANES:(at + 1) * LANES, columns_at] = (
                    ref[block * LANES:(block + 1) * LANES, columns_at] * spread
                )
            at += 1


def normed(columns, powers, blocks):
    rows = sum(block.shape[0] for block in blocks)
    width = blocks[0].shape[1]
    return pl.pallas_call(
        functools.partial(norm_kernel, columns, len(powers)),
        in_specs=[vmem()] * (len(powers) + len(blocks)),
        out_specs=vmem(),
        out_shape=jax.ShapeDtypeStruct((rows, width), jnp.float32),
        cost_estimate=cost(rows * width, 8 * rows * width),
        compiler_params=params(),
    )(*powers, *blocks)


def square_lanes(first_factor, second_factor, result_in, pivot_scale):
    return square_lanes_body(first_factor, second_factor, result_in, pivot_scale)


def square_lanes_body(first_factor, second_factor, result_in, pivot_scale):
    bands, lanes = lax.axis_size("band"), lax.axis_size("lane")
    chips = bands // CORES
    band, lane = lax.axis_index("band"), lax.axis_index("lane")
    where = jnp.stack([band // CORES, band % CORES, lane]).astype(jnp.int32)

    def send(axis, perm, value):
        return lax.ppermute(value, axis, perm)

    def across(distance):
        return [(l, l ^ distance) for l in range(lanes)]

    def px(value):
        return send("lane", across(1), value)

    def py(value):
        return send("lane", across(2), value)

    def pd(value):
        return send("lane", across(3), value)

    up = [(b, (b + CORES) % bands) for b in range(bands)]
    swap = [(b, b ^ 1) for b in range(bands)]

    lane_at = where[2:]
    own_t0, own_b0 = scaled_pieces(lane_at, first_factor, pivot_scale, 0, 2, 2)
    own_t1, own_b1 = scaled_pieces(lane_at, first_factor, pivot_scale, 1, 2, 2)

    mine = [second_factor]
    for _ in range(1, chips):
        mine.append(send("band", up, mine[-1]))
    other = [send("band", swap, piece) for piece in mine]

    x_t0, y_b0 = px(own_t0), py(own_b0)
    x_b0, y_t0 = px(own_b0), py(own_t0)
    x_t1, y_b1 = px(own_t1), py(own_b1)
    d_b0, d_t0 = px(y_b0), py(x_t0)
    x_b1, y_t1 = px(own_b1), py(own_t1)
    d_b1, d_t1 = px(y_b1), py(x_t1)

    right = laid(where, mine, other)
    lefts = [own_t0, own_b0, own_t1, own_b1, x_t0, x_b0, x_t1, y_t0, y_b0, y_b1]
    plan = [
        [(0, 0), (4, 1), (7, 2)],
        [(1, 0), (5, 1), (8, 2)],
        [(2, 0), (6, 1)],
        [(3, 0), (9, 2)],
    ]
    t0, b0, t1, b1 = first_products(where, right, result_in, lefts, plan)
    t0, b0, t1, b1 = products(
        where, right, [t0, b0, t1, b1], [d_t0, d_b0, y_t1, x_b1],
        [[(0, 3)], [(1, 3)], [(2, 2)], [(3, 1)]],
    )
    (t1, b1), power = last_products(
        where, right, [t0, b0], [t1, b1], [d_t1, d_b1], [[(0, 3)], [(1, 3)]]
    )
    columns = result_in.shape[1] * lanes
    powers = [power, px(power), py(power), pd(power)]
    return normed(columns, powers, [t0, b0, t1, b1])


def any_lanes(first_factor, second_factor, result_in, pivot_scale):
    share = first_factor.shape[1]
    part_scale = lax.dynamic_slice_in_dim(pivot_scale, lax.axis_index("lane") * share, share)
    scaled_left = (first_factor.astype(jnp.float32) * part_scale).astype(jnp.bfloat16)
    left_line = lax.all_gather(scaled_left, "lane", axis=1, tiled=True)
    right_line = lax.all_gather(second_factor, "band", axis=0, tiled=True)
    total = jnp.dot(left_line, right_line, preferred_element_type=jnp.float32)
    updated = result_in - total
    row_power = lax.psum(jnp.sum(updated * updated, axis=1), "lane")
    columns = updated.shape[1] * lax.axis_size("lane")
    return updated * lax.rsqrt(row_power / columns + EPS)[:, None]


def solution(mesh):
    square = mesh.shape["lane"] == 4 and mesh.shape["band"] == 4 * CORES
    return jax.shard_map(
        square_lanes if square else any_lanes,
        mesh=mesh,
        in_specs=(P("band", "lane"), P("band", "lane"), P("band", "lane"), P()),
        out_specs=P("band", "lane"),
        check_vma=False,
    )
```

time: 177 us -> 106 us (0.60)
  waiting for transfers between devices: 133 us -> 50.8 us
  Pallas kernels: 0 us -> 30.8 us
  starting transfers between devices: 0.04 us -> 21.3 us
  between operations: 13.4 us -> 0.16 us
  matrix products: 11.1 us -> 0 us
  blocking collectives: 8.9 us -> 0 us
  other arithmetic: 5.32 us -> 0.61 us
  local copies, waits for them, and re-layouts: 5.88 us -> 2.24 us
    all_gather x2 -> x0, waiting for transfers between devices: 132 us -> none  [the longest x1 88.2 us: on_device(): left_line = lax.all_gather(scaled_left, 'lane', axis=1, tiled=True)]
    ppermute x0 -> x22, waiting for transfers between devices: none -> 50.8 us  [send(): return lax.ppermute(value, axis, perm)]
    pallas_call x0 -> x7, Pallas kernels: none -> 30.8 us  [the longest x1 7.97 us: first_products(): pl.pallas_call(functools.partial(first_kernel, plan), in_specs=[pl.BlockS...]
    ppermute x0 -> x22, starting transfers between devices: none -> 21.3 us  [send(): return lax.ppermute(value, axis, perm)]
    dot_general x1 -> x0, matrix products: 11.1 us -> none  [join_panel(): return jnp.dot(left_panel, right_panel, preferred_element_type=jnp.float32)]
    psum x1 -> x0, blocking collectives: 8.9 us -> none  [on_device(): row_power = lax.psum(jnp.sum(updated * updated, axis=1), 'lane')]
    convert_element_type x1 -> x0, other arithmetic: 3.49 us -> none  [on_device(): (first_factor.astype(jnp.float32) * part_scale).astype(jnp.bfloat16)]
    mul x1 -> x0, other arithmetic: 1.81 us -> none  [on_device(): updated * lax.rsqrt(row_power / (updated.shape[1] * lax.axis_size('lane')...]
  transfers between devices with their start and end apart: 2 -> 22, of which waited for: 2 -> 10; matrix products, arithmetic and copies ran while one was open for 3% -> 1% of each run, Pallas kernels for 0% -> 22%
where the time goes in v1:
time: 106 us
  waiting for transfers between devices  50.8 us (48%)
  Pallas kernels  30.8 us (29%)
  starting transfers between devices  21.3 us (20%)
  local copies, waits for them, and re-layouts  2.24 us (2%)
    ppermute x22, waiting for transfers between devices, send(): return lax.ppermute(value, axis, perm)  50.8 us
    ppermute x22, starting transfers between devices, send(): return lax.ppermute(value, axis, perm)  21.3 us
    pallas_call x1, Pallas kernels, first_products(): pl.pallas_call(functools.partial(first_kernel, plan), in_specs=[pl.BlockS...  7.97 us
    pallas_call x1, Pallas kernels, products(): pl.pallas_call(functools.partial(product_kernel, plan, 0), in_specs=[pl.B...  5.42 us
    pallas_call x2, Pallas kernels, scaled_pieces(): pl.pallas_call(scale_kernel, grid_spec=pltpu.PrefetchScalarGridSpec(num_s...  4.91 us
    pallas_call x1, Pallas kernels, laid(): pl.pallas_call(functools.partial(lay_kernel, chips), in_specs=[pl.BlockSp...  4.84 us
    pallas_call x1, Pallas kernels, last_products(): pl.pallas_call(functools.partial(last_kernel, plan, len(done)), in_specs=...  4.57 us
    pallas_call x1, Pallas kernels, normed(): pl.pallas_call(functools.partial(norm_kernel, columns, len(powers)), in_s...  3.07 us
  transfers between devices with their start and end apart: 22, of which 10 were waited for; matrix products, arithmetic and copies ran while one was open for 1% of the time, Pallas kernels for 22%

profile of v1, /device:TPU:0, one launch (start us, length us, event | category | flops | bytes accessed | tf_op | source)
XLA Modules:
  0.0 105.8 jit_solution(7590116942994511520)
XLA Ops:
  0.0 3.1 %collective-permute-start = (bf16[512,512]{1,0:T(8,128)(2,1)}, bf16[512,512]{1,0:T(8,128)(2,1)S(1)}, u32[]{:S(2)}, u32[]{:S(2)}) collective-permute-start(bf16[512,512]{1,0:T(8,128)(2,1)} %refs_0_.1), channel_id=1, source_target_pairs={{0,8},{4,12},{8,16},{12,20},{16,24},{20,28},{24,0},{28,4},{1,9},{5... | collective-permute-start | bytes 1572872 | tf_op jit(solution)/shard_map/ppermute | solution.py:222
  3.1 2.3 %shard_map.47 = (bf16[256,1024]{1,0:T(8,128)(2,1)}, bf16[256,1024]{1,0:T(8,128)(2,1)}) custom-call(s32[1]{0:T(128)} %bitcast.2.lane_ref, bf16[1024,1024]{1,0:T(8,128)(2,1)} %left_ref.3, f32[4096]{0:T(1024)} %scale_ref.3), custom_call_target="tpu_custom_call" | custom-call | flops 1048576 | bytes 2097152 | tf_op jit(solution)/shard_map/pallas_call | solution.py:41
  5.4 1.5 %collective-permute-start.11 = (bf16[256,1024]{1,0:T(8,128)(2,1)}, bf16[256,1024]{1,0:T(8,128)(2,1)S(1)}, u32[]{:S(2)}, u32[]{:S(2)}) collective-permute-start(bf16[256,1024]{1,0:T(8,128)(2,1)} %get-tuple-element.21.refs_1_), channel_id=1, source_target_pairs={{0,2},{1,3},{2,0},{3,1},{4,6},{5,7},{6,4},{7,5},{8,10},{9,11},{10,... | collective-permute-start | bytes 1572872 | tf_op jit(solution)/shard_map/ppermute | solution.py:222
  6.9 10.3 %collective-permute-done.refs_1_ = bf16[512,512]{1,0:T(8,128)(2,1)S(1)} collective-permute-done((bf16[512,512]{1,0:T(8,128)(2,1)}, bf16[512,512]{1,0:T(8,128)(2,1)S(1)}, u32[]{:S(2)}, u32[]{:S(2)}) %collective-permute-start) | collective-permute-done | bytes 524320 | tf_op jit(solution)/shard_map/ppermute | solution.py:222
  17.2 2.6 %shard_map.48 = (bf16[256,1024]{1,0:T(8,128)(2,1)}, bf16[256,1024]{1,0:T(8,128)(2,1)}) custom-call(s32[1]{0:T(128)} %bitcast.2.lane_ref, bf16[1024,1024]{1,0:T(8,128)(2,1)} %left_ref.3, f32[4096]{0:T(1024)} %scale_ref.3), custom_call_target="tpu_custom_call" | custom-call | flops 1048576 | bytes 2097152 | tf_op jit(solution)/shard_map/pallas_call | solution.py:41
  19.8 1.5 %collective-permute-start.12 = (bf16[256,1024]{1,0:T(8,128)(2,1)}, bf16[256,1024]{1,0:T(8,128)(2,1)S(1)}, u32[]{:S(2)}, u32[]{:S(2)}) collective-permute-start(bf16[256,1024]{1,0:T(8,128)(2,1)} %get-tuple-element.23.refs_3_), channel_id=1, source_target_pairs={{0,2},{1,3},{2,0},{3,1},{4,6},{5,7},{6,4},{7,5},{8,10},{9,11},{10,... | collective-permute-start | bytes 1572872 | tf_op jit(solution)/shard_map/ppermute | solution.py:222
  21.3 1.5 %collective-permute-start.7 = (bf16[256,1024]{1,0:T(8,128)(2,1)S(1)}, bf16[256,1024]{1,0:T(8,128)(2,1)}, u32[]{:S(2)}, u32[]{:S(2)}) collective-permute-start(bf16[256,1024]{1,0:T(8,128)(2,1)S(1)} %copy-done.2), channel_id=1, source_target_pairs={{0,1},{1,0},{2,3},{3,2},{4,5},{5,4},{6,7},{7,6},{8,9},{9,8},{10,11... | collective-permute-start | bytes 1572872 | tf_op jit(solution)/shard_map/ppermute | solution.py:222
  22.8 0.8 copy-done.6
  24.6 7.5 %collective-permute-done.1.refs_2_ = bf16[512,512]{1,0:T(8,128)(2,1)S(1)} collective-permute-done((bf16[512,512]{1,0:T(8,128)(2,1)S(1)}, bf16[512,512]{1,0:T(8,128)(2,1)S(1)}, u32[]{:S(2)}, u32[]{:S(2)}) %collective-permute-start.1) | collective-permute-done | bytes 524320 | tf_op jit(solution)/shard_map/ppermute | solution.py:222
  32.1 2.7 %collective-permute-done.12.refs_9_ = bf16[256,1024]{1,0:T(8,128)(2,1)S(1)} collective-permute-done((bf16[256,1024]{1,0:T(8,128)(2,1)}, bf16[256,1024]{1,0:T(8,128)(2,1)S(1)}, u32[]{:S(2)}, u32[]{:S(2)}) %collective-permute-start.12) | collective-permute-done | bytes 524320 | tf_op jit(solution)/shard_map/ppermute | solution.py:222
  34.8 1.5 %collective-permute-start.8 = (bf16[256,1024]{1,0:T(8,128)(2,1)S(1)}, bf16[256,1024]{1,0:T(8,128)(2,1)S(1)}, u32[]{:S(2)}, u32[]{:S(2)}) collective-permute-start(bf16[256,1024]{1,0:T(8,128)(2,1)S(1)} %copy-done.3), channel_id=1, source_target_pairs={{0,1},{1,0},{2,3},{3,2},{4,5},{5,4},{6,7},{7,6},{8,9},{9,8},{10,11... | collective-permute-start | bytes 1572872 | tf_op jit(solution)/shard_map/ppermute | solution.py:222
  36.3 1.5 %collective-permute-start.15 = (bf16[256,1024]{1,0:T(8,128)(2,1)}, bf16[256,1024]{1,0:T(8,128)(2,1)S(1)}, u32[]{:S(2)}, u32[]{:S(2)}) collective-permute-start(bf16[256,1024]{1,0:T(8,128)(2,1)} %get-tuple-element.22.refs_2_), channel_id=1, source_target_pairs={{0,2},{1,3},{2,0},{3,1},{4,6},{5,7},{6,4},{7,5},{8,10},{9,11},{10,... | collective-permute-start | bytes 1572872 | tf_op jit(solution)/shard_map/ppermute | solution.py:222
  37.8 9.5 %collective-permute-done.9.refs_6_ = bf16[256,1024]{1,0:T(8,128)(2,1)S(1)} collective-permute-done((bf16[256,1024]{1,0:T(8,128)(2,1)}, bf16[256,1024]{1,0:T(8,128)(2,1)S(1)}, u32[]{:S(2)}, u32[]{:S(2)}) %collective-permute-start.9) | collective-permute-done | bytes 524320 | tf_op jit(solution)/shard_map/ppermute | solution.py:222
  47.9 8.4 %collective-permute-done.8.refs_5_ = bf16[256,1024]{1,0:T(8,128)(2,1)S(1)} collective-permute-done((bf16[256,1024]{1,0:T(8,128)(2,1)S(1)}, bf16[256,1024]{1,0:T(8,128)(2,1)S(1)}, u32[]{:S(2)}, u32[]{:S(2)}) %collective-permute-start.8) | collective-permute-done | bytes 524320 | tf_op jit(solution)/shard_map/ppermute | solution.py:222
  56.4 1.5 %collective-permute-start.16 = (bf16[256,1024]{1,0:T(8,128)(2,1)}, bf16[256,1024]{1,0:T(8,128)(2,1)S(1)}, u32[]{:S(2)}, u32[]{:S(2)}) collective-permute-start(bf16[256,1024]{1,0:T(8,128)(2,1)} %get-tuple-element.23.refs_3_), channel_id=1, source_target_pairs={{0,1},{1,0},{2,3},{3,2},{4,5},{5,4},{6,7},{7,6},{8,9},{9,8},{10,11... | collective-permute-start | bytes 1572872 | tf_op jit(solution)/shard_map/ppermute | solution.py:222
  58.4 0.8 collective-permute-start.14
  59.1 1.3 %collective-permute-start.17 = (bf16[256,1024]{1,0:T(8,128)(2,1)S(1)}, bf16[256,1024]{1,0:T(8,128)(2,1)}, u32[]{:S(2)}, u32[]{:S(2)}) collective-permute-start(bf16[256,1024]{1,0:T(8,128)(2,1)S(1)} %collective-permute-done.9.refs_6_), channel_id=1, source_target_pairs={{0,2},{1,3},{2,0},{3,1},{4,6},{5,7},{6,4},{7,5},{8,10},{9,11},{10,... | collective-permute-start | bytes 1572872 | tf_op jit(solution)/shard_map/ppermute | solution.py:222
  60.5 0.8 copy-done.16
  61.3 1.5 %collective-permute-start.18 = (bf16[256,1024]{1,0:T(8,128)(2,1)S(1)}, bf16[256,1024]{1,0:T(8,128)(2,1)}, u32[]{:S(2)}, u32[]{:S(2)}) collective-permute-start(bf16[256,1024]{1,0:T(8,128)(2,1)S(1)} %collective-permute-done.12.refs_9_), channel_id=1, source_target_pairs={{0,1},{1,0},{2,3},{3,2},{4,5},{5,4},{6,7},{7,6},{8,9},{9,8},{10,11... | collective-permute-start | bytes 1572872 | tf_op jit(solution)/shard_map/ppermute | solution.py:222
  62.8 0.6 pad_add_fusion.where_ref
  63.4 4.8 %shard_map.46.right_ref = bf16[4096,512]{1,0:T(8,128)(2,1)} custom-call(s32[3]{0:T(128)} %pad_add_fusion.where_ref, bf16[512,512]{1,0:T(8,128)(2,1)} %refs_0_.1, bf16[512,512]{1,0:T(8,128)(2,1)} %copy-done.4, bf16[512,512]{1,0:T(8,128)(2,1)} %copy-done.7, bf16[512,512]{1,0:T(8,128)(2,1)} %copy-done.11, bf16[512,512]{1,0:T(8,128)(2,1)} %copy-done.6, ...), custom_call_target="tpu_custom_call" | custom-call | flops 2097152 | bytes 8388608 | tf_op jit(solution)/shard_map/pallas_call | solution.py:80
  68.3 8.0 %shard_map.49 = (f32[256,512]{1,0:T(8,128)}, f32[256,512]{1,0:T(8,128)}, f32[256,512]{1,0:T(8,128)}, f32[256,512]{1,0:T(8,128)}) custom-call(s32[3]{0:T(128)} %pad_add_fusion.where_ref, bf16[4096,512]{1,0:T(8,128)(2,1)} %shard_map.46.right_ref, f32[1024,512]{1,0:T(8,128)} %base_ref.1, bf16[256,1024]{1,0:T(8,128)(2,1)} %get-tuple-element.20.refs_0_, ...), custom_call_target="tpu_custom_call" | custom-call | flops 2684354560 | bytes 5242880 | tf_op jit(solution)/shard_map/pallas_call | solution.py:140
  76.3 6.4 %collective-permute-done.14.refs_5_ = bf16[256,1024]{1,0:T(8,128)(2,1)} collective-permute-done((bf16[256,1024]{1,0:T(8,128)(2,1)S(1)}, bf16[256,1024]{1,0:T(8,128)(2,1)}, u32[]{:S(2)}, u32[]{:S(2)}) %collective-permute-start.14) | collective-permute-done | bytes 524320 | tf_op jit(solution)/shard_map/ppermute | solution.py:222
  82.7 5.4 %shard_map.50 = (f32[256,512]{1,0:T(8,128)}, f32[256,512]{1,0:T(8,128)}, f32[256,512]{1,0:T(8,128)}, f32[256,512]{1,0:T(8,128)}) custom-call(s32[3]{0:T(128)} %pad_add_fusion.where_ref, bf16[4096,512]{1,0:T(8,128)(2,1)} %shard_map.46.right_ref, f32[256,512]{1,0:T(8,128)} %get-tuple-element.24.refs_0_, f32[256,512]{1,0:T(8,128)} %get-tuple-element.25.refs_1_, ...), custom_call_target="tpu_custom_call" | custom-call | flops 1073741824 | bytes 2097152 | tf_op jit(solution)/shard_map/pallas_call | solution.py:121
  88.1 2.7 %collective-permute-done.18.refs_5_ = bf16[256,1024]{1,0:T(8,128)(2,1)} collective-permute-done((bf16[256,1024]{1,0:T(8,128)(2,1)S(1)}, bf16[256,1024]{1,0:T(8,128)(2,1)}, u32[]{:S(2)}, u32[]{:S(2)}) %collective-permute-start.18) | collective-permute-done | bytes 524320 | tf_op jit(solution)/shard_map/ppermute | solution.py:222
  90.9 4.6 %shard_map.51 = (f32[256,512]{1,0:T(8,128)}, f32[256,512]{1,0:T(8,128)}, f32[8,128]{1,0:T(8,128)}) custom-call(s32[3]{0:T(128)} %pad_add_fusion.where_ref, bf16[4096,512]{1,0:T(8,128)(2,1)} %shard_map.46.right_ref, f32[256,512]{1,0:T(8,128)} %get-tuple-element.28.refs_0_.refs_4_, f32[256,512]{1,0:T(8,128)} %get-tuple-element.29.refs_1_.refs_5_, ...), custom_call_target="tpu_custom_call" | custom-call | flops 536870912 | bytes 1048576 | tf_op jit(solution)/shard_map/pallas_call | solution.py:167
  95.5 1.5 %collective-permute-start.19 = (f32[8,128]{1,0:T(8,128)}, f32[8,128]{1,0:T(8,128)S(1)}, u32[]{:S(2)}, u32[]{:S(2)}) collective-permute-start(f32[8,128]{1,0:T(8,128)} %get-tuple-element.32.refs_0_), channel_id=1, source_target_pairs={{0,1},{1,0},{2,3},{3,2},{4,5},{5,4},{6,7},{7,6},{8,9},{9,8},{10,11... | collective-permute-start | bytes 12296 | tf_op jit(solution)/shard_map/ppermute | solution.py:222
  97.5 1.5 %collective-permute-start.21 = (f32[8,128]{1,0:T(8,128)}, f32[8,128]{1,0:T(8,128)S(1)}, u32[]{:S(2)}, u32[]{:S(2)}) collective-permute-start(f32[8,128]{1,0:T(8,128)} %get-tuple-element.32.refs_0_), channel_id=1, source_target_pairs={{0,3},{1,2},{2,1},{3,0},{4,7},{5,6},{6,5},{7,4},{8,11},{9,10},{10,... | collective-permute-start | bytes 12296 | tf_op jit(solution)/shard_map/ppermute | solution.py:222
  99.3 1.5 %collective-permute-done.20.refs_2_ = f32[8,128]{1,0:T(8,128)S(1)} collective-permute-done((f32[8,128]{1,0:T(8,128)}, f32[8,128]{1,0:T(8,128)S(1)}, u32[]{:S(2)}, u32[]{:S(2)}) %collective-permute-start.20) | collective-permute-done | bytes 4128 | tf_op jit(solution)/shard_map/ppermute | solution.py:222
  100.8 1.4 %collective-permute-done.21.refs_3_ = f32[8,128]{1,0:T(8,128)S(1)} collective-permute-done((f32[8,128]{1,0:T(8,128)}, f32[8,128]{1,0:T(8,128)S(1)}, u32[]{:S(2)}, u32[]{:S(2)}) %collective-permute-start.21) | collective-permute-done | bytes 4128 | tf_op jit(solution)/shard_map/ppermute | solution.py:222
  102.2 0.6 copy-done.19
  102.8 3.1 %shard_map.52 = f32[1024,512]{1,0:T(8,128)} custom-call(f32[8,128]{1,0:T(8,128)} %get-tuple-element.32.refs_0_, f32[8,128]{1,0:T(8,128)} %copy-done.17, f32[8,128]{1,0:T(8,128)} %copy-done.18, f32[8,128]{1,0:T(8,128)} %copy-done.19, f32[256,512]{1,0:T(8,128)} %get-tuple-element.28.refs_0_.refs_4_, f32[256,512]{1,0:T(8,128)} %get-tuple-element.29.refs_1_.refs_5_, ...), custom_call_target="tpu_custom_call" | custom-call | flops 524288 | bytes 4194304 | tf_op jit(solution)/shard_map/pallas_call | solution.py:201
  (60 shorter events, 3.1 us)
Async XLA Ops:
  0.0 17.2 %collective-permute-start = (bf16[512,512]{1,0:T(8,128)(2,1)}, bf16[512,512]{1,0:T(8,128)(2,1)S(1)}, u32[]{:S(2)}, u32[]{:S(2)}) collective-permute-start(bf16[512,512]{1,0:T(8,128)(2,1)} %refs_0_.1), channel_id=1, source_target_pairs={{0,8},{4,12},{8,16},{12,20},{16,24},{20,28},{24,0},{28,4},{1,9},{5... | collective-permute-start | bytes 1572872 | tf_op jit(solution)/shard_map/ppermute | solution.py:222
  3.1 19.7 %collective-permute-start.3 = (bf16[512,512]{1,0:T(8,128)(2,1)}, bf16[512,512]{1,0:T(8,128)(2,1)S(1)}, u32[]{:S(2)}, u32[]{:S(2)}) collective-permute-start(bf16[512,512]{1,0:T(8,128)(2,1)} %refs_0_.1), channel_id=1, source_target_pairs={{0,4},{4,0},{8,12},{12,8},{16,20},{20,16},{24,28},{28,24},{1,5},{5... | collective-permute-start | bytes 1572872 | tf_op jit(solution)/shard_map/ppermute | solution.py:222
  5.4 15.9 %copy-start.2 = (bf16[256,1024]{1,0:T(8,128)(2,1)S(1)}, bf16[256,1024]{1,0:T(8,128)(2,1)}, u32[]{:S(2)}) copy-start(bf16[256,1024]{1,0:T(8,128)(2,1)} %get-tuple-element.20.refs_0_) | copy-start | bytes 1572868
  5.4 29.4 %copy-start.3 = (bf16[256,1024]{1,0:T(8,128)(2,1)S(1)}, bf16[256,1024]{1,0:T(8,128)(2,1)}, u32[]{:S(2)}) copy-start(bf16[256,1024]{1,0:T(8,128)(2,1)} %get-tuple-element.21.refs_1_) | copy-start | bytes 1572868
  5.4 18.7 %collective-permute-start.11 = (bf16[256,1024]{1,0:T(8,128)(2,1)}, bf16[256,1024]{1,0:T(8,128)(2,1)S(1)}, u32[]{:S(2)}, u32[]{:S(2)}) collective-permute-start(bf16[256,1024]{1,0:T(8,128)(2,1)} %get-tuple-element.21.refs_1_), channel_id=1, source_target_pairs={{0,2},{1,3},{2,0},{3,1},{4,6},{5,7},{6,4},{7,5},{8,10},{9,11},{10,... | collective-permute-start | bytes 1572872 | tf_op jit(solution)/shard_map/ppermute | solution.py:222
  17.2 46.2 %copy-start.4 = (bf16[512,512]{1,0:T(8,128)(2,1)}, bf16[512,512]{1,0:T(8,128)(2,1)S(1)}, u32[]{:S(2)}) copy-start(bf16[512,512]{1,0:T(8,128)(2,1)S(1)} %collective-permute-done.refs_1_) | copy-start | bytes 1572868
  17.2 14.9 %collective-permute-start.1 = (bf16[512,512]{1,0:T(8,128)(2,1)S(1)}, bf16[512,512]{1,0:T(8,128)(2,1)S(1)}, u32[]{:S(2)}, u32[]{:S(2)}) collective-permute-start(bf16[512,512]{1,0:T(8,128)(2,1)S(1)} %collective-permute-done.refs_1_), channel_id=1, source_target_pairs={{0,8},{4,12},{8,16},{12,20},{16,24},{20,28},{24,0},{28,4},{1,9},{5... | collective-permute-start | bytes 1572872 | tf_op jit(solution)/shard_map/ppermute | solution.py:222
  19.8 15.0 %collective-permute-start.12 = (bf16[256,1024]{1,0:T(8,128)(2,1)}, bf16[256,1024]{1,0:T(8,128)(2,1)S(1)}, u32[]{:S(2)}, u32[]{:S(2)}) collective-permute-start(bf16[256,1024]{1,0:T(8,128)(2,1)} %get-tuple-element.23.refs_3_), channel_id=1, source_target_pairs={{0,2},{1,3},{2,0},{3,1},{4,6},{5,7},{6,4},{7,5},{8,10},{9,11},{10,... | collective-permute-start | bytes 1572872 | tf_op jit(solution)/shard_map/ppermute | solution.py:222
  21.3 15.0 %collective-permute-start.7 = (bf16[256,1024]{1,0:T(8,128)(2,1)S(1)}, bf16[256,1024]{1,0:T(8,128)(2,1)}, u32[]{:S(2)}, u32[]{:S(2)}) collective-permute-start(bf16[256,1024]{1,0:T(8,128)(2,1)S(1)} %copy-done.2), channel_id=1, source_target_pairs={{0,1},{1,0},{2,3},{3,2},{4,5},{5,4},{6,7},{7,6},{8,9},{9,8},{10,11... | collective-permute-start | bytes 1572872 | tf_op jit(solution)/shard_map/ppermute | solution.py:222
  23.6 23.7 %collective-permute-start.9 = (bf16[256,1024]{1,0:T(8,128)(2,1)}, bf16[256,1024]{1,0:T(8,128)(2,1)S(1)}, u32[]{:S(2)}, u32[]{:S(2)}) collective-permute-start(bf16[256,1024]{1,0:T(8,128)(2,1)} %get-tuple-element.22.refs_2_), channel_id=1, source_target_pairs={{0,1},{1,0},{2,3},{3,2},{4,5},{5,4},{6,7},{7,6},{8,9},{9,8},{10,11... | collective-permute-start | bytes 1572872 | tf_op jit(solution)/shard_map/ppermute | solution.py:222
  24.1 44.1 %copy-start.1 = (bf16[256,1024]{1,0:T(8,128)(2,1)}, bf16[256,1024]{1,0:T(8,128)(2,1)S(1)}, u32[]{:S(2)}) copy-start(bf16[256,1024]{1,0:T(8,128)(2,1)S(1)} %collective-permute-done.11.refs_8_) | copy-start | bytes 1572868
  24.1 23.2 %collective-permute-start.10 = (bf16[256,1024]{1,0:T(8,128)(2,1)S(1)}, bf16[256,1024]{1,0:T(8,128)(2,1)S(1)}, u32[]{:S(2)}, u32[]{:S(2)}) collective-permute-start(bf16[256,1024]{1,0:T(8,128)(2,1)S(1)} %copy-done.2), channel_id=1, source_target_pairs={{0,2},{1,3},{2,0},{3,1},{4,6},{5,7},{6,4},{7,5},{8,10},{9,11},{10,... | collective-permute-start | bytes 1572872 | tf_op jit(solution)/shard_map/ppermute | solution.py:222
  32.1 28.3 %copy-start.7 = (bf16[512,512]{1,0:T(8,128)(2,1)}, bf16[512,512]{1,0:T(8,128)(2,1)S(1)}, u32[]{:S(2)}) copy-start(bf16[512,512]{1,0:T(8,128)(2,1)S(1)} %collective-permute-done.1.refs_2_) | copy-start | bytes 1572868
  32.1 15.7 %collective-permute-start.2 = (bf16[512,512]{1,0:T(8,128)(2,1)S(1)}, bf16[512,512]{1,0:T(8,128)(2,1)S(1)}, u32[]{:S(2)}, u32[]{:S(2)}) collective-permute-start(bf16[512,512]{1,0:T(8,128)(2,1)S(1)} %collective-permute-done.1.refs_2_), channel_id=1, source_target_pairs={{0,8},{4,12},{8,16},{12,20},{16,24},{20,28},{24,0},{28,4},{1,9},{5... | collective-permute-start | bytes 1572872 | tf_op jit(solution)/shard_map/ppermute | solution.py:222
  34.8 33.5 %copy-start = (bf16[256,1024]{1,0:T(8,128)(2,1)}, bf16[256,1024]{1,0:T(8,128)(2,1)S(1)}, u32[]{:S(2)}) copy-start(bf16[256,1024]{1,0:T(8,128)(2,1)S(1)} %collective-permute-done.12.refs_9_) | copy-start | bytes 1572868
  34.8 21.6 %collective-permute-start.8 = (bf16[256,1024]{1,0:T(8,128)(2,1)S(1)}, bf16[256,1024]{1,0:T(8,128)(2,1)S(1)}, u32[]{:S(2)}, u32[]{:S(2)}) collective-permute-start(bf16[256,1024]{1,0:T(8,128)(2,1)S(1)} %copy-done.3), channel_id=1, source_target_pairs={{0,1},{1,0},{2,3},{3,2},{4,5},{5,4},{6,7},{7,6},{8,9},{9,8},{10,11... | collective-permute-start | bytes 1572872 | tf_op jit(solution)/shard_map/ppermute | solution.py:222
  36.3 21.6 %collective-permute-start.15 = (bf16[256,1024]{1,0:T(8,128)(2,1)}, bf16[256,1024]{1,0:T(8,128)(2,1)S(1)}, u32[]{:S(2)}, u32[]{:S(2)}) collective-permute-start(bf16[256,1024]{1,0:T(8,128)(2,1)} %get-tuple-element.22.refs_2_), channel_id=1, source_target_pairs={{0,2},{1,3},{2,0},{3,1},{4,6},{5,7},{6,4},{7,5},{8,10},{9,11},{10,... | collective-permute-start | bytes 1572872 | tf_op jit(solution)/shard_map/ppermute | solution.py:222
  47.3 20.9 %copy-start.5 = (bf16[256,1024]{1,0:T(8,128)(2,1)}, bf16[256,1024]{1,0:T(8,128)(2,1)S(1)}, u32[]{:S(2)}) copy-start(bf16[256,1024]{1,0:T(8,128)(2,1)S(1)} %collective-permute-done.9.refs_6_) | copy-start | bytes 1572868
  47.3 11.0 %collective-permute-start.4 = (bf16[512,512]{1,0:T(8,128)(2,1)S(1)}, bf16[512,512]{1,0:T(8,128)(2,1)S(1)}, u32[]{:S(2)}, u32[]{:S(2)}) collective-permute-start(bf16[512,512]{1,0:T(8,128)(2,1)S(1)} %collective-permute-done.refs_1_), channel_id=1, source_target_pairs={{0,4},{4,0},{8,12},{12,8},{16,20},{20,16},{24,28},{28,24},{1,5},{5... | collective-permute-start | bytes 1572872 | tf_op jit(solution)/shard_map/ppermute | solution.py:222
  47.3 13.1 %copy-start.8 = (bf16[256,1024]{1,0:T(8,128)(2,1)}, bf16[256,1024]{1,0:T(8,128)(2,1)S(1)}, u32[]{:S(2)}) copy-start(bf16[256,1024]{1,0:T(8,128)(2,1)S(1)} %collective-permute-done.10.refs_7_) | copy-start | bytes 1572868
  47.3 11.8 %collective-permute-start.5 = (bf16[512,512]{1,0:T(8,128)(2,1)S(1)}, bf16[512,512]{1,0:T(8,128)(2,1)S(1)}, u32[]{:S(2)}, u32[]{:S(2)}) collective-permute-start(bf16[512,512]{1,0:T(8,128)(2,1)S(1)} %collective-permute-done.1.refs_2_), channel_id=1, source_target_pairs={{0,4},{4,0},{8,12},{12,8},{16,20},{20,16},{24,28},{28,24},{1,5},{5... | collective-permute-start | bytes 1572872 | tf_op jit(solution)/shard_map/ppermute | solution.py:222
  47.9 12.6 %copy-start.11 = (bf16[512,512]{1,0:T(8,128)(2,1)}, bf16[512,512]{1,0:T(8,128)(2,1)S(1)}, u32[]{:S(2)}) copy-start(bf16[512,512]{1,0:T(8,128)(2,1)S(1)} %collective-permute-done.2.refs_3_) | copy-start | bytes 1572868
  47.9 12.6 %collective-permute-start.6 = (bf16[512,512]{1,0:T(8,128)(2,1)S(1)}, bf16[512,512]{1,0:T(8,128)(2,1)S(1)}, u32[]{:S(2)}, u32[]{:S(2)}) collective-permute-start(bf16[512,512]{1,0:T(8,128)(2,1)S(1)} %collective-permute-done.2.refs_3_), channel_id=1, source_target_pairs={{0,4},{4,0},{8,12},{12,8},{16,20},{20,16},{24,28},{28,24},{1,5},{5... | collective-permute-start | bytes 1572872 | tf_op jit(solution)/shard_map/ppermute | solution.py:222
  56.4 19.9 %collective-permute-start.16 = (bf16[256,1024]{1,0:T(8,128)(2,1)}, bf16[256,1024]{1,0:T(8,128)(2,1)S(1)}, u32[]{:S(2)}, u32[]{:S(2)}) collective-permute-start(bf16[256,1024]{1,0:T(8,128)(2,1)} %get-tuple-element.23.refs_3_), channel_id=1, source_target_pairs={{0,1},{1,0},{2,3},{3,2},{4,5},{5,4},{6,7},{7,6},{8,9},{9,8},{10,11... | collective-permute-start | bytes 1572872 | tf_op jit(solution)/shard_map/ppermute | solution.py:222
  57.9 18.4 %collective-permute-start.13 = (bf16[256,1024]{1,0:T(8,128)(2,1)}, bf16[256,1024]{1,0:T(8,128)(2,1)S(1)}, u32[]{:S(2)}, u32[]{:S(2)}) collective-permute-start(bf16[256,1024]{1,0:T(8,128)(2,1)} %collective-permute-done.7.refs_4_), channel_id=1, source_target_pairs={{0,2},{1,3},{2,0},{3,1},{4,6},{5,7},{6,4},{7,5},{8,10},{9,11},{10,... | collective-permute-start | bytes 1572872 | tf_op jit(solution)/shard_map/ppermute | solution.py:222
  58.4 24.3 %collective-permute-start.14 = (bf16[256,1024]{1,0:T(8,128)(2,1)S(1)}, bf16[256,1024]{1,0:T(8,128)(2,1)}, u32[]{:S(2)}, u32[]{:S(2)}) collective-permute-start(bf16[256,1024]{1,0:T(8,128)(2,1)S(1)} %collective-permute-done.11.refs_8_), channel_id=1, source_target_pairs={{0,1},{1,0},{2,3},{3,2},{4,5},{5,4},{6,7},{7,6},{8,9},{9,8},{10,11... | collective-permute-start | bytes 1572872 | tf_op jit(solution)/shard_map/ppermute | solution.py:222
  59.1 29.0 %collective-permute-start.17 = (bf16[256,1024]{1,0:T(8,128)(2,1)S(1)}, bf16[256,1024]{1,0:T(8,128)(2,1)}, u32[]{:S(2)}, u32[]{:S(2)}) collective-permute-start(bf16[256,1024]{1,0:T(8,128)(2,1)S(1)} %collective-permute-done.9.refs_6_), channel_id=1, source_target_pairs={{0,2},{1,3},{2,0},{3,1},{4,6},{5,7},{6,4},{7,5},{8,10},{9,11},{10,... | collective-permute-start | bytes 1572872 | tf_op jit(solution)/shard_map/ppermute | solution.py:222
  61.3 29.6 %collective-permute-start.18 = (bf16[256,1024]{1,0:T(8,128)(2,1)S(1)}, bf16[256,1024]{1,0:T(8,128)(2,1)}, u32[]{:S(2)}, u32[]{:S(2)}) collective-permute-start(bf16[256,1024]{1,0:T(8,128)(2,1)S(1)} %collective-permute-done.12.refs_9_), channel_id=1, source_target_pairs={{0,1},{1,0},{2,3},{3,2},{4,5},{5,4},{6,7},{7,6},{8,9},{9,8},{10,11... | collective-permute-start | bytes 1572872 | tf_op jit(solution)/shard_map/ppermute | solution.py:222
  76.3 6.5 %copy-start.12 = (bf16[256,1024]{1,0:T(8,128)(2,1)}, bf16[256,1024]{1,0:T(8,128)(2,1)S(1)}, u32[]{:S(2)}) copy-start(bf16[256,1024]{1,0:T(8,128)(2,1)S(1)} %collective-permute-done.16.refs_7_) | copy-start | bytes 1572868
  95.5 3.8 %collective-permute-start.19 = (f32[8,128]{1,0:T(8,128)}, f32[8,128]{1,0:T(8,128)S(1)}, u32[]{:S(2)}, u32[]{:S(2)}) collective-permute-start(f32[8,128]{1,0:T(8,128)} %get-tuple-element.32.refs_0_), channel_id=1, source_target_pairs={{0,1},{1,0},{2,3},{3,2},{4,5},{5,4},{6,7},{7,6},{8,9},{9,8},{10,11... | collective-permute-start | bytes 12296 | tf_op jit(solution)/shard_map/ppermute | solution.py:222
  96.9 3.8 %collective-permute-start.20 = (f32[8,128]{1,0:T(8,128)}, f32[8,128]{1,0:T(8,128)S(1)}, u32[]{:S(2)}, u32[]{:S(2)}) collective-permute-start(f32[8,128]{1,0:T(8,128)} %get-tuple-element.32.refs_0_), channel_id=1, source_target_pairs={{0,2},{1,3},{2,0},{3,1},{4,6},{5,7},{6,4},{7,5},{8,10},{9,11},{10,... | collective-permute-start | bytes 12296 | tf_op jit(solution)/shard_map/ppermute | solution.py:222
  97.5 4.7 %collective-permute-start.21 = (f32[8,128]{1,0:T(8,128)}, f32[8,128]{1,0:T(8,128)S(1)}, u32[]{:S(2)}, u32[]{:S(2)}) collective-permute-start(f32[8,128]{1,0:T(8,128)} %get-tuple-element.32.refs_0_), channel_id=1, source_target_pairs={{0,3},{1,2},{2,1},{3,0},{4,7},{5,6},{6,5},{7,4},{8,11},{9,10},{10,... | collective-permute-start | bytes 12296 | tf_op jit(solution)/shard_map/ppermute | solution.py:222
  (10 other events, 23.1 us)

commit v2 on v0

v2 whole, which is shorter than its diff:
```python
import functools

import jax
import jax.numpy as jnp
from jax import lax
from jax.experimental import pallas as pl
from jax.experimental.pallas import tpu as pltpu
from jax.sharding import PartitionSpec as P


CORES = 2
EPS = 1e-06
LANES = 128
MIB = 1024 * 1024


def cost(flops, nbytes):
    return pl.CostEstimate(flops=int(flops), bytes_accessed=int(nbytes), transcendentals=0)


def vmem():
    return pl.BlockSpec(memory_space=pltpu.VMEM)


def params(mib):
    return pltpu.CompilerParams(vmem_limit_bytes=mib * MIB)


def smem():
    return pl.BlockSpec(memory_space=pltpu.SMEM)


def scale_kernel(lane_ref, left_ref, scale_ref, *outs):
    scale = scale_ref[...].reshape(1, -1)
    height = outs[0].shape[0]
    for at, out in enumerate(outs):
        rows = left_ref[at * height:(at + 1) * height, :]
        out[...] = (rows.astype(jnp.float32) * scale).astype(jnp.bfloat16)


def scaled_pieces(lane, left, scale, block, blocks, count):
    rows, depth = left.shape
    height = rows // blocks
    piece = jax.ShapeDtypeStruct((height // count, depth), jnp.bfloat16)
    return pl.pallas_call(
        scale_kernel,
        grid_spec=pltpu.PrefetchScalarGridSpec(
            num_scalar_prefetch=1,
            grid=(1,),
            in_specs=[
                pl.BlockSpec((height, depth), lambda i, lane: (block, 0)),
                pl.BlockSpec((depth,), lambda i, lane: (lane[0],)),
            ],
            out_specs=[pl.BlockSpec(piece.shape, lambda i, lane: (0, 0))] * count,
        ),
        out_shape=[piece] * count,
        cost_estimate=cost(2 * height * depth, 4 * height * depth),
        compiler_params=params(60),
    )(lane, left, scale)


def bring(where_ref, first, agreeing, others, out, sems):
    z, core, lane, agree = where_ref[0], where_ref[1], where_ref[2], where_ref[3]

    def both(pieces):
        copies = []
        for at, (distance, mine, other) in enumerate(pieces):
            depth = mine.shape[0]
            ahead = lax.bitwise_xor(z, distance) == lax.bitwise_xor(lane, first)
            slot = jnp.where(ahead, 0, CORES * depth)
            for part, (source, half) in enumerate(((mine, core), (other, 1 - core))):
                start = pl.multiple_of(slot + half * depth, depth)
                copies.append(
                    pltpu.make_async_copy(source, out.at[pl.ds(start, depth), :], sems.at[at, part])
                )
        for copy in copies:
            copy.start()
        for copy in copies:
            copy.wait()

    @pl.when(agree == 1)
    def _():
        both(agreeing)

    @pl.when(agree == 0)
    def _():
        both(others)


def split(pieces):
    distances = [distance for distance, _ in pieces]
    arrays = [array for _, pair in pieces for array in pair]

    def joined_again(refs):
        rows = [(distances[at], *refs[2 * at:2 * at + 2]) for at in range(4)]
        return rows[:2], rows[2:]

    return arrays, joined_again


def block_of(pieces):
    depth, width = pieces[0][1][0].shape
    return jax.ShapeDtypeStruct((2 * CORES * depth, width), jnp.bfloat16)


def bring_one(where_ref, agreeing, others, out, sems):
    core, agree = where_ref[1], where_ref[3]

    def one(pair):
        copies = []
        for part, (source, half) in enumerate(((pair[0], core), (pair[1], 1 - core))):
            depth = source.shape[0]
            start = pl.multiple_of(half * depth, depth)
            copies.append(
                pltpu.make_async_copy(source, out.at[pl.ds(start, depth), :], sems.at[part])
            )
        for copy in copies:
            copy.start()
        for copy in copies:
            copy.wait()

    @pl.when(agree == 1)
    def _():
        one(agreeing)

    @pl.when(agree == 0)
    def _():
        one(others)


def is_own(where_ref, distances):
    z, lane, agree = where_ref[0], where_ref[2], where_ref[3]
    distance = jnp.where(agree == 1, distances[0], distances[1])
    return lax.bitwise_xor(z, distance) == lane


def dot(left, right):
    return jnp.dot(left, right, preferred_element_type=jnp.float32)


def partial_first(where, pieces, own, side):
    arrays, again = split(pieces)
    block = block_of(pieces)
    rows, deep = own.shape
    width = block.shape[1]

    def kernel(where_ref, *refs):
        own_ref, side_ref, sent_ref, right_ref, sems = refs[8:]
        bring(where_ref, 0, *again(refs[:8]), right_ref, sems)
        total = dot(own_ref[...], right_ref[:deep, :]) + dot(side_ref[...], right_ref[deep:, :])
        sent_ref[...] = total.astype(jnp.bfloat16)

    return pl.pallas_call(
        kernel,
        in_specs=[smem()] + [pl.BlockSpec(memory_space=pl.ANY)] * 8 + [vmem()] * 2,
        out_specs=[vmem()] * 2,
        out_shape=[jax.ShapeDtypeStruct((rows, width), jnp.bfloat16), block],
        scratch_shapes=[pltpu.SemaphoreType.DMA((2, CORES))],
        cost_estimate=cost(4 * rows * deep * width, 4 * deep * width),
        compiler_params=params(16),
    )(where, *arrays, own, side)


def partial_kernel(count, right_ref, *refs):
    owns, sides, outs = refs[:count], refs[count:2 * count], refs[2 * count:]
    deep = owns[0].shape[1]
    for own, side, out in zip(owns, sides, outs):
        total = dot(own[...], right_ref[:deep, :]) + dot(side[...], right_ref[deep:, :])
        out[...] = total.astype(jnp.bfloat16)


def partials(right, owns, sides):
    count = len(owns)
    rows, deep = owns[0].shape
    width = right.shape[1]
    return pl.pallas_call(
        functools.partial(partial_kernel, count),
        in_specs=[vmem()] * (1 + 2 * count),
        out_specs=[vmem()] * count,
        out_shape=[jax.ShapeDtypeStruct((rows, width), jnp.bfloat16)] * count,
        cost_estimate=cost(4 * count * rows * deep * width, 4 * deep * width),
        compiler_params=params(20),
    )(right, *owns, *sides)


def kept(where, distances, pieces, base, owns, sides):
    count = len(owns)
    height, deep = owns[0].shape
    width = base.shape[1]

    def kernel(where_ref, *refs):
        base_ref, lefts = refs[4], refs[5:5 + 2 * count]
        outs, right_ref, sems = refs[5 + 2 * count:5 + 3 * count], refs[-2], refs[-1]
        bring_one(where_ref, refs[:2], refs[2:4], right_ref, sems)
        own = is_own(where_ref, distances)

        def products(chosen):
            for at in range(count):
                outs[at][...] = base_ref[at * height:(at + 1) * height, :] - dot(
                    chosen[at][...], right_ref[...]
                )

        pl.when(own)(lambda: products(lefts[:count]))
        pl.when(jnp.logical_not(own))(lambda: products(lefts[count:]))

    flops = 2 * count * height * deep * width
    return pl.pallas_call(
        kernel,
        in_specs=[smem()] + [pl.BlockSpec(memory_space=pl.ANY)] * 4 + [vmem()] * (1 + 2 * count),
        out_specs=[vmem()] * count,
        out_shape=[jax.ShapeDtypeStruct((height, width), jnp.float32)] * count,
        scratch_shapes=[
            pltpu.VMEM((deep, width), jnp.bfloat16), pltpu.SemaphoreType.DMA((CORES,))
        ],
        cost_estimate=cost(flops, flops / 512),
        compiler_params=params(24),
    )(where, *pieces[0], *pieces[1], base, *owns, *sides)


def power_rows(block):
    squares = block * block
    folded = squares[:, :LANES]
    for at in range(1, block.shape[1] // LANES):
        folded = folded + squares[:, at * LANES:(at + 1) * LANES]
    return jnp.sum(folded.T, axis=0, keepdims=True)


def put_powers(ref, power_ref, at):
    for block in range(ref.shape[0] // LANES):
        power_ref[at:at + 1, :] = power_rows(ref[block * LANES:(block + 1) * LANES, :])
        at += 1
    return at


def joined(where, distances, pieces, keeps, gots, owns, sides, before):
    count = len(keeps)
    height, deep = owns[0].shape
    width = keeps[0].shape[1]
    block = jax.ShapeDtypeStruct((deep, width), jnp.bfloat16)
    done = before[1].shape[0] if before else 0
    n_first = 2 if before else 4

    def kernel(where_ref, *refs):
        first, rest = refs[:n_first], refs[n_first:]
        kept_refs, got_refs, lefts = rest[:count], rest[count:2 * count], rest[2 * count:4 * count]
        outs, power_ref = rest[4 * count:5 * count], rest[5 * count]
        if before:
            right_ref = first[0]
            power_ref[:done, :] = first[1][...]
        else:
            right_ref = rest[5 * count + 1]
            bring_one(where_ref, first[:2], first[2:], right_ref, rest[5 * count + 2])
        own = is_own(where_ref, distances)

        def products(chosen):
            for at in range(count):
                total = dot(chosen[at][...], right_ref[...])
                outs[at][...] = kept_refs[at][...] - total - got_refs[at][...].astype(jnp.float32)

        pl.when(own)(lambda: products(lefts[:count]))
        pl.when(jnp.logical_not(own))(lambda: products(lefts[count:]))
        at = done
        for out in outs:
            at = put_powers(out, power_ref, at)

    flops = 2 * count * height * deep * width
    results = pl.pallas_call(
        kernel,
        in_specs=[smem()]
        + [vmem() if before else pl.BlockSpec(memory_space=pl.ANY)] * n_first
        + [vmem()] * (4 * count),
        out_specs=[vmem()] * (count + 1 + (not before)),
        out_shape=[jax.ShapeDtypeStruct((height, width), jnp.float32)] * count
        + [jax.ShapeDtypeStruct((done + count * height // LANES, LANES), jnp.float32)]
        + ([] if before else [block]),
        scratch_shapes=[] if before else [pltpu.SemaphoreType.DMA((CORES,))],
        cost_estimate=cost(flops, flops / 256),
        compiler_params=params(16),
    )(where, *(before if before else (*pieces[0], *pieces[1])), *keeps, *gots, *owns, *sides)
    return results[:count], results[count], None if before else results[count + 1]


def norm_kernel(columns, n_power, *refs):
    powers, blocks, out = refs[:n_power], refs[n_power:-1], refs[-1]
    power = powers[0][...]
    for ref in powers[1:]:
        power = power + ref[...]
    factor = lax.rsqrt(power / columns + EPS)
    at = 0
    for ref in blocks:
        for block in range(ref.shape[0] // LANES):
            spread = jnp.broadcast_to(factor[at:at + 1, :], (LANES, LANES)).T
            for tile in range(ref.shape[1] // LANES):
                columns_at = slice(tile * LANES, (tile + 1) * LANES)
                out[at * LANES:(at + 1) * LANES, columns_at] = (
                    ref[block * LANES:(block + 1) * LANES, columns_at] * spread
                )
            at += 1


def normed(columns, powers, blocks):
    rows = sum(block.shape[0] for block in blocks)
    width = blocks[0].shape[1]
    return pl.pallas_call(
        functools.partial(norm_kernel, columns, len(powers)),
        in_specs=[vmem()] * (len(powers) + len(blocks)),
        out_specs=vmem(),
        out_shape=jax.ShapeDtypeStruct((rows, width), jnp.float32),
        cost_estimate=cost(rows * width, 8 * rows * width),
        compiler_params=params(8),
    )(*powers, *blocks)


def square_lanes(first_factor, second_factor, result_in, pivot_scale):
    return square_lanes_body(first_factor, second_factor, result_in, pivot_scale)


def square_lanes_body(first_factor, second_factor, result_in, pivot_scale):
    bands, lanes = lax.axis_size("band"), lax.axis_size("lane")
    chips = bands // CORES
    band, lane = lax.axis_index("band"), lax.axis_index("lane")
    z, core = band // CORES, band % CORES
    agree = jnp.where(z % 2 == lane % 2, 1, 0)
    where = jnp.stack([z, core, lane, agree]).astype(jnp.int32)

    def send(axis, perm, value):
        return lax.ppermute(value, axis, perm)

    def across(distance):
        return [(l, l ^ distance) for l in range(lanes)]

    def some(target, wanted):
        pairs = []
        for b in range(bands):
            for l in range(lanes):
                if ((b // CORES) % 2 == l % 2) == wanted:
                    to_b, to_l = target(b, l)
                    pairs.append((b * lanes + l, to_b * lanes + to_l))
        return pairs

    both = ("band", "lane")
    swap = [(b, b ^ 1) for b in range(bands)]

    def px(value):
        return send("lane", across(1), value)

    def py(value):
        return send("lane", across(2), value)

    def swapped(value):
        return value, send("band", swap, value)

    def to_plane(distance):
        return lambda b, l: (b ^ (CORES * distance), l)

    def to_side(distance):
        return lambda b, l: (b ^ (CORES * distance), l ^ 1)

    r0 = second_factor
    side = [swapped(send(both, some(to_side(at), False), r0)) for at in range(chips)]
    line = [(r0, None)] + [
        swapped(send(both, some(to_plane(at), True), r0))
        for at in range(1, chips)
    ]
    at_hand = (swapped(r0), line[1])
    later = (line[2], line[3])
    far = [(0, side[0]), (2, side[2]), (1, side[1]), (3, side[3])]

    lane_at = where[2:3]
    owns = [
        *scaled_pieces(lane_at, first_factor, pivot_scale, 0, 2, 2),
        *scaled_pieces(lane_at, first_factor, pivot_scale, 1, 2, 2),
    ]
    sides = [py(own) for own in owns]

    sent0, far_right = partial_first(where, far, owns[0], sides[0])
    sents = [sent0]
    for own, side in zip(owns[1:], sides[1:]):
        sents += partials(far_right, [own], [side])
    backs = [px(sent) for sent in sents]

    keeps = kept(where, (0, 1), at_hand, result_in, owns, sides)
    n = len(owns) - 1
    outs, power, late_right = joined(
        where, (2, 3), later, keeps[:n], backs[:n], owns[:n], sides[:n], ()
    )
    last_outs, power, _ = joined(
        where, (2, 3), later, keeps[n:], backs[n:], owns[n:], sides[n:], (late_right, power)
    )
    outs = [*outs, *last_outs]
    columns = result_in.shape[1] * lanes
    powers = [power, px(power), py(power), send("lane", across(3), power)]
    return normed(columns, powers, outs)


def any_lanes(first_factor, second_factor, result_in, pivot_scale):
    share = first_factor.shape[1]
    part_scale = lax.dynamic_slice_in_dim(pivot_scale, lax.axis_index("lane") * share, share)
    scaled_left = (first_factor.astype(jnp.float32) * part_scale).astype(jnp.bfloat16)
    left_line = lax.all_gather(scaled_left, "lane", axis=1, tiled=True)
    right_line = lax.all_gather(second_factor, "band", axis=0, tiled=True)
    total = jnp.dot(left_line, right_line, preferred_element_type=jnp.float32)
    updated = result_in - total
    row_power = lax.psum(jnp.sum(updated * updated, axis=1), "lane")
    columns = updated.shape[1] * lax.axis_size("lane")
    return updated * lax.rsqrt(row_power / columns + EPS)[:, None]


def solution(mesh):
    square = mesh.shape["lane"] == 4 and mesh.shape["band"] == 4 * CORES
    return jax.shard_map(
        square_lanes if square else any_lanes,
        mesh=mesh,
        in_specs=(P("band", "lane"), P("band", "lane"), P("band", "lane"), P()),
        out_specs=P("band", "lane"),
        check_vma=False,
    )
```

time: 177 us -> 128 us (0.72)
  waiting for transfers between devices: 133 us -> 59.5 us
  starting transfers between devices: 0.04 us -> 41.3 us
  Pallas kernels: 0 us -> 16.6 us
  between operations: 13.4 us -> 0.23 us
  matrix products: 11.1 us -> 0 us
  blocking collectives: 8.9 us -> 0 us
  other arithmetic: 5.32 us -> 0.08 us
  local copies, waits for them, and re-layouts: 5.88 us -> 9.87 us
    all_gather x2 -> x0, waiting for transfers between devices: 132 us -> none  [the longest x1 88.2 us: on_device(): left_line = lax.all_gather(scaled_left, 'lane', axis=1, tiled=True)]
    ppermute x0 -> x26, waiting for transfers between devices: none -> 59.5 us  [send(): return lax.ppermute(value, axis, perm)]
    ppermute x0 -> x26, starting transfers between devices: none -> 41.3 us  [send(): return lax.ppermute(value, axis, perm)]
    pallas_call x0 -> x10, Pallas kernels: none -> 16.6 us  [the longest x2 4.7 us: scaled_pieces(): pl.pallas_call(scale_kernel, grid_spec=pltpu.PrefetchScalarGridSpec(num_s...]
    dot_general x1 -> x0, matrix products: 11.1 us -> none  [join_panel(): return jnp.dot(left_panel, right_panel, preferred_element_type=jnp.float32)]
    psum x1 -> x0, blocking collectives: 8.9 us -> none  [on_device(): row_power = lax.psum(jnp.sum(updated * updated, axis=1), 'lane')]
    unnamed x3 -> x40, local copies, waits for them, and re-layouts: 3.37 us -> 9.87 us
    convert_element_type x1 -> x0, other arithmetic: 3.49 us -> none  [on_device(): (first_factor.astype(jnp.float32) * part_scale).astype(jnp.bfloat16)]
  transfers between devices with their start and end apart: 2 -> 26, of which waited for: 2 -> 12; matrix products, arithmetic and copies ran while one was open for 3% -> 0% of each run, Pallas kernels for 0% -> 11%
where the time goes in v2:
time: 128 us; the launch traced here: 127 us
  waiting for transfers between devices  59.5 us (46%)
  starting transfers between devices  41.3 us (32%)
  Pallas kernels  16.6 us (13%)
  local copies, waits for them, and re-layouts  9.87 us (8%)
    ppermute x26, waiting for transfers between devices, send(): return lax.ppermute(value, axis, perm)  59.5 us
    ppermute x26, starting transfers between devices, send(): return lax.ppermute(value, axis, perm)  41.3 us
    unnamed x40, local copies, waits for them, and re-layouts  9.87 us
    pallas_call x2, Pallas kernels, scaled_pieces(): pl.pallas_call(scale_kernel, grid_spec=pltpu.PrefetchScalarGridSpec(num_s...  4.7 us
    pallas_call x2, Pallas kernels, joined(): pl.pallas_call(kernel, in_specs=[smem()] + [vmem() if before else pl.Bloc...  3.89 us
    pallas_call x1, Pallas kernels, kept(): pl.pallas_call(kernel, in_specs=[smem()] + [pl.BlockSpec(memory_space=pl....  2.89 us
  transfers between devices with their start and end apart: 26, of which 12 were waited for; matrix products, arithmetic and copies ran while one was open for 0% of the time, Pallas kernels for 11%

profile of v2, /device:TPU:0, one launch (start us, length us, event | category | flops | bytes accessed | tf_op | source)
XLA Modules:
  0.0 127.5 jit_solution(5559473771348029865)
XLA Ops:
  0.0 1.3 %collective-permute-start.13 = (bf16[512,512]{1,0:T(8,128)(2,1)}, bf16[512,512]{1,0:T(8,128)(2,1)S(1)}, u32[]{:S(2)}, u32[]{:S(2)}) collective-permute-start(bf16[512,512]{1,0:T(8,128)(2,1)} %refs_0_.1), channel_id=1, source_target_pairs={{1,16},{3,18},{5,20},{7,22},{8,25},{10,27},{12,29},{14,31},{17,0},... | collective-permute-start | bytes 1572872 | tf_op jit(solution)/shard_map/ppermute | solution.py:327
  1.3 1.3 %collective-permute-start.11 = (bf16[512,512]{1,0:T(8,128)(2,1)}, bf16[512,512]{1,0:T(8,128)(2,1)S(1)}, u32[]{:S(2)}, u32[]{:S(2)}) collective-permute-start(bf16[512,512]{1,0:T(8,128)(2,1)} %refs_0_.1), channel_id=1, source_target_pairs={{1,0},{3,2},{5,4},{7,6},{8,9},{10,11},{12,13},{14,15},{17,16},{19,... | collective-permute-start | bytes 1572872 | tf_op jit(solution)/shard_map/ppermute | solution.py:327
  2.6 10.0 %collective-permute-start.5 = (bf16[512,512]{1,0:T(8,128)(2,1)}, bf16[512,512]{1,0:T(8,128)(2,1)}, u32[]{:S(2)}, u32[]{:S(2)}) collective-permute-start(bf16[512,512]{1,0:T(8,128)(2,1)} %refs_0_.1), channel_id=1, source_target_pairs={{0,8},{2,10},{4,12},{6,14},{9,1},{11,3},{13,5},{15,7},{16,24},{18,... | collective-permute-start | bytes 1572872 | tf_op jit(solution)/shard_map/ppermute | solution.py:327
  12.6 1.3 %collective-permute-start.2 = (bf16[512,512]{1,0:T(8,128)(2,1)}, bf16[512,512]{1,0:T(8,128)(2,1)S(1)}, u32[]{:S(2)}, u32[]{:S(2)}) collective-permute-start(bf16[512,512]{1,0:T(8,128)(2,1)} %refs_0_.1), channel_id=1, source_target_pairs={{0,24},{2,26},{4,28},{6,30},{9,17},{11,19},{13,21},{15,23},{16,8},... | collective-permute-start | bytes 1572872 | tf_op jit(solution)/shard_map/ppermute | solution.py:327
  13.9 2.6 %collective-permute-start = (bf16[512,512]{1,0:T(8,128)(2,1)}, bf16[512,512]{1,0:T(8,128)(2,1)}, u32[]{:S(2)}, u32[]{:S(2)}) collective-permute-start(bf16[512,512]{1,0:T(8,128)(2,1)} %refs_0_.1), channel_id=1, source_target_pairs={{0,16},{2,18},{4,20},{6,22},{9,25},{11,27},{13,29},{15,31},{16,0},... | collective-permute-start | bytes 1572872 | tf_op jit(solution)/shard_map/ppermute | solution.py:327
  16.5 2.1 %collective-permute-done.13.refs_2_ = bf16[512,512]{1,0:T(8,128)(2,1)S(1)} collective-permute-done((bf16[512,512]{1,0:T(8,128)(2,1)}, bf16[512,512]{1,0:T(8,128)(2,1)S(1)}, u32[]{:S(2)}, u32[]{:S(2)}) %collective-permute-start.13) | collective-permute-done | bytes 524320 | tf_op jit(solution)/shard_map/ppermute | solution.py:327
  18.5 1.5 %collective-permute-start.17 = (bf16[512,512]{1,0:T(8,128)(2,1)}, bf16[512,512]{1,0:T(8,128)(2,1)}, u32[]{:S(2)}, u32[]{:S(2)}) collective-permute-start(bf16[512,512]{1,0:T(8,128)(2,1)} %refs_0_.1), channel_id=1, source_target_pairs={{1,24},{3,26},{5,28},{7,30},{8,17},{10,19},{12,21},{14,23},{17,8},... | collective-permute-start | bytes 1572872 | tf_op jit(solution)/shard_map/ppermute | solution.py:327
  20.0 9.6 %collective-permute-done.11.refs_0_ = bf16[512,512]{1,0:T(8,128)(2,1)S(1)} collective-permute-done((bf16[512,512]{1,0:T(8,128)(2,1)}, bf16[512,512]{1,0:T(8,128)(2,1)S(1)}, u32[]{:S(2)}, u32[]{:S(2)}) %collective-permute-start.11) | collective-permute-done | bytes 524320 | tf_op jit(solution)/shard_map/ppermute | solution.py:327
  29.6 1.5 %collective-permute-start.15 = (bf16[512,512]{1,0:T(8,128)(2,1)}, bf16[512,512]{1,0:T(8,128)(2,1)}, u32[]{:S(2)}, u32[]{:S(2)}) collective-permute-start(bf16[512,512]{1,0:T(8,128)(2,1)} %refs_0_.1), channel_id=1, source_target_pairs={{1,8},{3,10},{5,12},{7,14},{8,1},{10,3},{12,5},{14,7},{17,24},{19,... | collective-permute-start | bytes 1572872 | tf_op jit(solution)/shard_map/ppermute | solution.py:327
  31.1 2.4 %shard_map.47 = (bf16[256,1024]{1,0:T(8,128)(2,1)}, bf16[256,1024]{1,0:T(8,128)(2,1)}) custom-call(s32[1]{0:T(128)} %bitcast.2.lane_ref, bf16[1024,1024]{1,0:T(8,128)(2,1)} %left_ref.3, f32[4096]{0:T(1024)} %scale_ref.3), custom_call_target="tpu_custom_call" | custom-call | flops 1048576 | bytes 2097152 | tf_op jit(solution)/shard_map/pallas_call | solution.py:45
  33.5 2.2 %collective-permute-start.9 = (bf16[256,1024]{1,0:T(8,128)(2,1)}, bf16[256,1024]{1,0:T(8,128)(2,1)S(1)}, u32[]{:S(2)}, u32[]{:S(2)}) collective-permute-start(bf16[256,1024]{1,0:T(8,128)(2,1)} %get-tuple-element.24.refs_7_.refs_0_.refs_12_), channel_id=1, source_target_pairs={{0,2},{1,3},{2,0},{3,1},{4,6},{5,7},{6,4},{7,5},{8,10},{9,11},{10,... | collective-permute-start | bytes 1572872 | tf_op jit(solution)/shard_map/ppermute | solution.py:327
  35.7 2.3 %shard_map.46 = (bf16[256,1024]{1,0:T(8,128)(2,1)}, bf16[256,1024]{1,0:T(8,128)(2,1)}) custom-call(s32[1]{0:T(128)} %bitcast.2.lane_ref, bf16[1024,1024]{1,0:T(8,128)(2,1)} %left_ref.3, f32[4096]{0:T(1024)} %scale_ref.3), custom_call_target="tpu_custom_call" | custom-call | flops 1048576 | bytes 2097152 | tf_op jit(solution)/shard_map/pallas_call | solution.py:45
  38.9 15.1 %collective-permute-done.refs_0_ = bf16[512,512]{1,0:T(8,128)(2,1)} collective-permute-done((bf16[512,512]{1,0:T(8,128)(2,1)}, bf16[512,512]{1,0:T(8,128)(2,1)}, u32[]{:S(2)}, u32[]{:S(2)}) %collective-permute-start) | collective-permute-done | bytes 524320 | tf_op jit(solution)/shard_map/ppermute | solution.py:327
  54.0 1.5 %collective-permute-start.8 = (bf16[256,1024]{1,0:T(8,128)(2,1)}, bf16[256,1024]{1,0:T(8,128)(2,1)S(1)}, u32[]{:S(2)}, u32[]{:S(2)}) collective-permute-start(bf16[256,1024]{1,0:T(8,128)(2,1)} %get-tuple-element.23.refs_6_.refs_0_.refs_11_), channel_id=1, source_target_pairs={{0,2},{1,3},{2,0},{3,1},{4,6},{5,7},{6,4},{7,5},{8,10},{9,11},{10,... | collective-permute-start | bytes 1572872 | tf_op jit(solution)/shard_map/ppermute | solution.py:327
  56.2 3.8 %collective-permute-done.7.refs_9_.refs_13_ = bf16[256,1024]{1,0:T(8,128)(2,1)S(1)} collective-permute-done((bf16[256,1024]{1,0:T(8,128)(2,1)}, bf16[256,1024]{1,0:T(8,128)(2,1)S(1)}, u32[]{:S(2)}, u32[]{:S(2)}) %collective-permute-start.7) | collective-permute-done | bytes 524320 | tf_op jit(solution)/shard_map/ppermute | solution.py:327
  59.9 10.6 %collective-permute-done.8.refs_10_.refs_1_.refs_14_ = bf16[256,1024]{1,0:T(8,128)(2,1)S(1)} collective-permute-done((bf16[256,1024]{1,0:T(8,128)(2,1)}, bf16[256,1024]{1,0:T(8,128)(2,1)S(1)}, u32[]{:S(2)}, u32[]{:S(2)}) %collective-permute-start.8) | collective-permute-done | bytes 524320 | tf_op jit(solution)/shard_map/ppermute | solution.py:327
  71.3 1.7 %collective-permute-start.10 = (bf16[256,1024]{1,0:T(8,128)(2,1)S(1)}, bf16[256,1024]{1,0:T(8,128)(2,1)S(1)}, u32[]{:S(2)}, u32[]{:S(2)}) collective-permute-start(bf16[256,1024]{1,0:T(8,128)(2,1)S(1)} %copy-done), channel_id=1, source_target_pairs={{0,2},{1,3},{2,0},{3,1},{4,6},{5,7},{6,4},{7,5},{8,10},{9,11},{10,... | collective-permute-start | bytes 1572872 | tf_op jit(solution)/shard_map/ppermute | solution.py:327
  75.6 1.0 copy-done.3
  81.8 1.4 %shard_map.49 = (bf16[256,512]{1,0:T(8,128)(2,1)S(1)}, bf16[2048,512]{1,0:T(8,128)(2,1)S(1)}) custom-call(s32[4]{0:T(128)S(1)} %pad_add_fusion.where_ref, bf16[512,512]{1,0:T(8,128)(2,1)S(1)} %copy-done.11, bf16[512,512]{1,0:T(8,128)(2,1)S(1)} %copy-done.15, bf16[512,512]{1,0:T(8,128)(2,1)S(1)} %copy-done.8, bf16[512,512]{1,0:T(8,128)(2,1)S(1)} %copy-done.13, ...), custom_call_target="tpu_custom_call" | custom-call | flops 536870912 | bytes 2097152 | tf_op jit(solution)/shard_map/pallas_call | solution.py:153
  85.1 9.3 %collective-permute-start.21 = (bf16[256,512]{1,0:T(8,128)(2,1)S(1)}, bf16[256,512]{1,0:T(8,128)(2,1)S(1)}, u32[]{:S(2)}, u32[]{:S(2)}) collective-permute-start(bf16[256,512]{1,0:T(8,128)(2,1)S(1)} %shard_map.51), channel_id=1, source_target_pairs={{0,1},{1,0},{2,3},{3,2},{4,5},{5,4},{6,7},{7,6},{8,9},{9,8},{10,11... | collective-permute-start | bytes 786440 | tf_op jit(solution)/shard_map/ppermute | solution.py:327
  94.4 1.9 %collective-permute-start.20 = (bf16[256,512]{1,0:T(8,128)(2,1)S(1)}, bf16[256,512]{1,0:T(8,128)(2,1)S(1)}, u32[]{:S(2)}, u32[]{:S(2)}) collective-permute-start(bf16[256,512]{1,0:T(8,128)(2,1)S(1)} %shard_map.50), channel_id=1, source_target_pairs={{0,1},{1,0},{2,3},{3,2},{4,5},{5,4},{6,7},{7,6},{8,9},{9,8},{10,11... | collective-permute-start | bytes 786440 | tf_op jit(solution)/shard_map/ppermute | solution.py:327
  97.3 2.9 %shard_map.48 = (f32[256,512]{1,0:T(8,128)S(1)}, f32[256,512]{1,0:T(8,128)S(1)}, f32[256,512]{1,0:T(8,128)S(1)}, f32[256,512]{1,0:T(8,128)S(1)}) custom-call(s32[4]{0:T(128)S(1)} %pad_add_fusion.where_ref, bf16[512,512]{1,0:T(8,128)(2,1)S(1)} %copy-done.6, bf16[512,512]{1,0:T(8,128)(2,1)} %collective-permute-done.4.refs_1_, ...), custom_call_target="tpu_custom_call" | custom-call | flops 1073741824 | bytes 2097152 | tf_op jit(solution)/shard_map/pallas_call | solution.py:207
  100.2 1.3 %collective-permute-done.21.refs_9_ = bf16[256,512]{1,0:T(8,128)(2,1)S(1)} collective-permute-done((bf16[256,512]{1,0:T(8,128)(2,1)S(1)}, bf16[256,512]{1,0:T(8,128)(2,1)S(1)}, u32[]{:S(2)}, u32[]{:S(2)}) %collective-permute-start.21) | collective-permute-done | bytes 262176 | tf_op jit(solution)/shard_map/ppermute | solution.py:327
  101.5 5.6 %collective-permute-done.19.refs_7_ = bf16[256,512]{1,0:T(8,128)(2,1)S(1)} collective-permute-done((bf16[256,512]{1,0:T(8,128)(2,1)S(1)}, bf16[256,512]{1,0:T(8,128)(2,1)S(1)}, u32[]{:S(2)}, u32[]{:S(2)}) %collective-permute-start.19) | collective-permute-done | bytes 262176 | tf_op jit(solution)/shard_map/ppermute | solution.py:327
  107.1 5.6 %collective-permute-done.20.refs_8_ = bf16[256,512]{1,0:T(8,128)(2,1)S(1)} collective-permute-done((bf16[256,512]{1,0:T(8,128)(2,1)S(1)}, bf16[256,512]{1,0:T(8,128)(2,1)S(1)}, u32[]{:S(2)}, u32[]{:S(2)}) %collective-permute-start.20) | collective-permute-done | bytes 262176 | tf_op jit(solution)/shard_map/ppermute | solution.py:327
  112.7 2.8 %shard_map.52 = (f32[256,512]{1,0:T(8,128)S(1)}, f32[256,512]{1,0:T(8,128)S(1)}, f32[256,512]{1,0:T(8,128)S(1)}, f32[6,128]{1,0:T(8,128)S(1)}, bf16[1024,512]{1,0:T(8,128)(2,1)S(1)}) custom-call(s32[4]{0:T(128)S(1)} %pad_add_fusion.where_ref, bf16[512,512]{1,0:T(8,128)(2,1)} %collective-permute-done.refs_0_, ...), custom_call_target="tpu_custom_call" | custom-call | flops 805306368 | bytes 3145728 | tf_op jit(solution)/shard_map/pallas_call | solution.py:267
  115.5 2.4 %collective-permute-done.22.refs_3_ = bf16[256,512]{1,0:T(8,128)(2,1)S(1)} collective-permute-done((bf16[256,512]{1,0:T(8,128)(2,1)S(1)}, bf16[256,512]{1,0:T(8,128)(2,1)S(1)}, u32[]{:S(2)}, u32[]{:S(2)}) %collective-permute-start.22) | collective-permute-done | bytes 262176 | tf_op jit(solution)/shard_map/ppermute | solution.py:327
  118.0 1.1 shard_map.54
  119.1 1.5 %collective-permute-start.25 = (f32[8,128]{1,0:T(8,128)S(1)}, f32[8,128]{1,0:T(8,128)S(1)}, u32[]{:S(2)}, u32[]{:S(2)}) collective-permute-start(f32[8,128]{1,0:T(8,128)S(1)} %get-tuple-element.34.refs_0_), channel_id=1, source_target_pairs={{0,3},{1,2},{2,1},{3,0},{4,7},{5,6},{6,5},{7,4},{8,11},{9,10},{10,... | collective-permute-start | bytes 12296 | tf_op jit(solution)/shard_map/ppermute | solution.py:327
  120.6 1.7 %collective-permute-start.24 = (f32[8,128]{1,0:T(8,128)S(1)}, f32[8,128]{1,0:T(8,128)S(1)}, u32[]{:S(2)}, u32[]{:S(2)}) collective-permute-start(f32[8,128]{1,0:T(8,128)S(1)} %get-tuple-element.34.refs_0_), channel_id=1, source_target_pairs={{0,2},{1,3},{2,0},{3,1},{4,6},{5,7},{6,4},{7,5},{8,10},{9,11},{10,... | collective-permute-start | bytes 12296 | tf_op jit(solution)/shard_map/ppermute | solution.py:327
  124.2 1.7 %collective-permute-done.23.refs_1_ = f32[8,128]{1,0:T(8,128)S(1)} collective-permute-done((f32[8,128]{1,0:T(8,128)S(1)}, f32[8,128]{1,0:T(8,128)S(1)}, u32[]{:S(2)}, u32[]{:S(2)}) %collective-permute-start.23) | collective-permute-done | bytes 4128 | tf_op jit(solution)/shard_map/ppermute | solution.py:327
  125.9 1.5 %shard_map.55 = f32[1024,512]{1,0:T(8,128)} custom-call(f32[8,128]{1,0:T(8,128)S(1)} %get-tuple-element.34.refs_0_, f32[8,128]{1,0:T(8,128)S(1)} %collective-permute-done.23.refs_1_, f32[8,128]{1,0:T(8,128)S(1)} %collective-permute-done.24.refs_2_, f32[8,128]{1,0:T(8,128)S(1)} %collective-permute-done.25.refs_3_, f32[256,512]{1,0:T(8,128)S(1)} %get-tuple-element.35.refs_4_, ...), custom_call_target="tpu_custom_call" | custom-call | flops 524288 | bytes 4194304 | tf_op jit(solution)/shard_map/pallas_call | solution.py:304
  (71 shorter events, 14.5 us)
Async XLA Ops:
  0.0 18.5 %collective-permute-start.13 = (bf16[512,512]{1,0:T(8,128)(2,1)}, bf16[512,512]{1,0:T(8,128)(2,1)S(1)}, u32[]{:S(2)}, u32[]{:S(2)}) collective-permute-start(bf16[512,512]{1,0:T(8,128)(2,1)} %refs_0_.1), channel_id=1, source_target_pairs={{1,16},{3,18},{5,20},{7,22},{8,25},{10,27},{12,29},{14,31},{17,0},... | collective-permute-start | bytes 1572872 | tf_op jit(solution)/shard_map/ppermute | solution.py:327
  1.3 28.3 %collective-permute-start.11 = (bf16[512,512]{1,0:T(8,128)(2,1)}, bf16[512,512]{1,0:T(8,128)(2,1)S(1)}, u32[]{:S(2)}, u32[]{:S(2)}) collective-permute-start(bf16[512,512]{1,0:T(8,128)(2,1)} %refs_0_.1), channel_id=1, source_target_pairs={{1,0},{3,2},{5,4},{7,6},{8,9},{10,11},{12,13},{14,15},{17,16},{19,... | collective-permute-start | bytes 1572872 | tf_op jit(solution)/shard_map/ppermute | solution.py:327
  2.6 30.9 %collective-permute-start.5 = (bf16[512,512]{1,0:T(8,128)(2,1)}, bf16[512,512]{1,0:T(8,128)(2,1)}, u32[]{:S(2)}, u32[]{:S(2)}) collective-permute-start(bf16[512,512]{1,0:T(8,128)(2,1)} %refs_0_.1), channel_id=1, source_target_pairs={{0,8},{2,10},{4,12},{6,14},{9,1},{11,3},{13,5},{15,7},{16,24},{18,... | collective-permute-start | bytes 1572872 | tf_op jit(solution)/shard_map/ppermute | solution.py:327
  12.6 25.5 %collective-permute-start.2 = (bf16[512,512]{1,0:T(8,128)(2,1)}, bf16[512,512]{1,0:T(8,128)(2,1)S(1)}, u32[]{:S(2)}, u32[]{:S(2)}) collective-permute-start(bf16[512,512]{1,0:T(8,128)(2,1)} %refs_0_.1), channel_id=1, source_target_pairs={{0,24},{2,26},{4,28},{6,30},{9,17},{11,19},{13,21},{15,23},{16,8},... | collective-permute-start | bytes 1572872 | tf_op jit(solution)/shard_map/ppermute | solution.py:327
  13.9 40.1 %collective-permute-start = (bf16[512,512]{1,0:T(8,128)(2,1)}, bf16[512,512]{1,0:T(8,128)(2,1)}, u32[]{:S(2)}, u32[]{:S(2)}) collective-permute-start(bf16[512,512]{1,0:T(8,128)(2,1)} %refs_0_.1), channel_id=1, source_target_pairs={{0,16},{2,18},{4,20},{6,22},{9,25},{11,27},{13,29},{15,31},{16,0},... | collective-permute-start | bytes 1572872 | tf_op jit(solution)/shard_map/ppermute | solution.py:327
  18.5 37.0 %copy-start.7 = (bf16[512,512]{1,0:T(8,128)(2,1)}, bf16[512,512]{1,0:T(8,128)(2,1)S(1)}, u32[]{:S(2)}) copy-start(bf16[512,512]{1,0:T(8,128)(2,1)S(1)} %collective-permute-done.13.refs_2_) | copy-start | bytes 1572868
  18.5 37.0 %collective-permute-start.17 = (bf16[512,512]{1,0:T(8,128)(2,1)}, bf16[512,512]{1,0:T(8,128)(2,1)}, u32[]{:S(2)}, u32[]{:S(2)}) collective-permute-start(bf16[512,512]{1,0:T(8,128)(2,1)} %refs_0_.1), channel_id=1, source_target_pairs={{1,24},{3,26},{5,28},{7,30},{8,17},{10,19},{12,21},{14,23},{17,8},... | collective-permute-start | bytes 1572872 | tf_op jit(solution)/shard_map/ppermute | solution.py:327
  29.6 25.9 %collective-permute-start.15 = (bf16[512,512]{1,0:T(8,128)(2,1)}, bf16[512,512]{1,0:T(8,128)(2,1)}, u32[]{:S(2)}, u32[]{:S(2)}) collective-permute-start(bf16[512,512]{1,0:T(8,128)(2,1)} %refs_0_.1), channel_id=1, source_target_pairs={{1,8},{3,10},{5,12},{7,14},{8,1},{10,3},{12,5},{14,7},{17,24},{19,... | collective-permute-start | bytes 1572872 | tf_op jit(solution)/shard_map/ppermute | solution.py:327
  31.1 39.4 %copy-start.6 = (bf16[512,512]{1,0:T(8,128)(2,1)S(1)}, bf16[512,512]{1,0:T(8,128)(2,1)}, u32[]{:S(2)}) copy-start(bf16[512,512]{1,0:T(8,128)(2,1)} %refs_0_.1) | copy-start | bytes 1572868
  33.5 22.1 %copy-start.10 = (bf16[512,512]{1,0:T(8,128)(2,1)S(1)}, bf16[512,512]{1,0:T(8,128)(2,1)}, u32[]{:S(2)}) copy-start(bf16[512,512]{1,0:T(8,128)(2,1)} %copy-done.9) | copy-start | bytes 1572868
  33.5 37.8 %copy-start = (bf16[256,1024]{1,0:T(8,128)(2,1)S(1)}, bf16[256,1024]{1,0:T(8,128)(2,1)}, u32[]{:S(2)}) copy-start(bf16[256,1024]{1,0:T(8,128)(2,1)} %get-tuple-element.25.refs_8_.refs_0_.refs_4_) | copy-start | bytes 1572868
  33.5 22.6 %collective-permute-start.9 = (bf16[256,1024]{1,0:T(8,128)(2,1)}, bf16[256,1024]{1,0:T(8,128)(2,1)S(1)}, u32[]{:S(2)}, u32[]{:S(2)}) collective-permute-start(bf16[256,1024]{1,0:T(8,128)(2,1)} %get-tuple-element.24.refs_7_.refs_0_.refs_12_), channel_id=1, source_target_pairs={{0,2},{1,3},{2,0},{3,1},{4,6},{5,7},{6,4},{7,5},{8,10},{9,11},{10,... | collective-permute-start | bytes 1572872 | tf_op jit(solution)/shard_map/ppermute | solution.py:327
  38.8 21.1 %collective-permute-start.7 = (bf16[256,1024]{1,0:T(8,128)(2,1)}, bf16[256,1024]{1,0:T(8,128)(2,1)S(1)}, u32[]{:S(2)}, u32[]{:S(2)}) collective-permute-start(bf16[256,1024]{1,0:T(8,128)(2,1)} %get-tuple-element.22.refs_5_.refs_8_.refs_10_), channel_id=1, source_target_pairs={{0,2},{1,3},{2,0},{3,1},{4,6},{5,7},{6,4},{7,5},{8,10},{9,11},{10,... | collective-permute-start | bytes 1572872 | tf_op jit(solution)/shard_map/ppermute | solution.py:327
  54.0 16.5 %collective-permute-start.8 = (bf16[256,1024]{1,0:T(8,128)(2,1)}, bf16[256,1024]{1,0:T(8,128)(2,1)S(1)}, u32[]{:S(2)}, u32[]{:S(2)}) collective-permute-start(bf16[256,1024]{1,0:T(8,128)(2,1)} %get-tuple-element.23.refs_6_.refs_0_.refs_11_), channel_id=1, source_target_pairs={{0,2},{1,3},{2,0},{3,1},{4,6},{5,7},{6,4},{7,5},{8,10},{9,11},{10,... | collective-permute-start | bytes 1572872 | tf_op jit(solution)/shard_map/ppermute | solution.py:327
  55.5 15.0 %collective-permute-start.14 = (bf16[512,512]{1,0:T(8,128)(2,1)S(1)}, bf16[512,512]{1,0:T(8,128)(2,1)S(1)}, u32[]{:S(2)}, u32[]{:S(2)}) collective-permute-start(bf16[512,512]{1,0:T(8,128)(2,1)S(1)} %collective-permute-done.13.refs_2_), channel_id=1, source_target_pairs={{0,4},{4,0},{8,12},{12,8},{16,20},{20,16},{24,28},{28,24},{1,5},{5... | collective-permute-start | bytes 1572872 | tf_op jit(solution)/shard_map/ppermute | solution.py:327
  55.6 17.5 %collective-permute-start.12 = (bf16[512,512]{1,0:T(8,128)(2,1)S(1)}, bf16[512,512]{1,0:T(8,128)(2,1)S(1)}, u32[]{:S(2)}, u32[]{:S(2)}) collective-permute-start(bf16[512,512]{1,0:T(8,128)(2,1)S(1)} %copy-done.10), channel_id=1, source_target_pairs={{0,4},{4,0},{8,12},{12,8},{16,20},{20,16},{24,28},{28,24},{1,5},{5... | collective-permute-start | bytes 1572872 | tf_op jit(solution)/shard_map/ppermute | solution.py:327
  56.1 18.1 %collective-permute-start.18 = (bf16[512,512]{1,0:T(8,128)(2,1)}, bf16[512,512]{1,0:T(8,128)(2,1)S(1)}, u32[]{:S(2)}, u32[]{:S(2)}) collective-permute-start(bf16[512,512]{1,0:T(8,128)(2,1)} %collective-permute-done.17.refs_6_), channel_id=1, source_target_pairs={{0,4},{4,0},{8,12},{12,8},{16,20},{20,16},{24,28},{28,24},{1,5},{5... | collective-permute-start | bytes 1572872 | tf_op jit(solution)/shard_map/ppermute | solution.py:327
  59.9 15.3 %collective-permute-start.16 = (bf16[512,512]{1,0:T(8,128)(2,1)}, bf16[512,512]{1,0:T(8,128)(2,1)}, u32[]{:S(2)}, u32[]{:S(2)}) collective-permute-start(bf16[512,512]{1,0:T(8,128)(2,1)} %collective-permute-done.15.refs_4_), channel_id=1, source_target_pairs={{0,4},{4,0},{8,12},{12,8},{16,20},{20,16},{24,28},{28,24},{1,5},{5... | collective-permute-start | bytes 1572872 | tf_op jit(solution)/shard_map/ppermute | solution.py:327
  70.5 14.5 %collective-permute-start.4 = (bf16[512,512]{1,0:T(8,128)(2,1)S(1)}, bf16[512,512]{1,0:T(8,128)(2,1)}, u32[]{:S(2)}, u32[]{:S(2)}) collective-permute-start(bf16[512,512]{1,0:T(8,128)(2,1)S(1)} %copy-done.6), channel_id=1, source_target_pairs={{0,4},{4,0},{8,12},{12,8},{16,20},{20,16},{24,28},{28,24},{1,5},{5... | collective-permute-start | bytes 1572872 | tf_op jit(solution)/shard_map/ppermute | solution.py:327
  71.3 23.0 %collective-permute-start.10 = (bf16[256,1024]{1,0:T(8,128)(2,1)S(1)}, bf16[256,1024]{1,0:T(8,128)(2,1)S(1)}, u32[]{:S(2)}, u32[]{:S(2)}) collective-permute-start(bf16[256,1024]{1,0:T(8,128)(2,1)S(1)} %copy-done), channel_id=1, source_target_pairs={{0,2},{1,3},{2,0},{3,1},{4,6},{5,7},{6,4},{7,5},{8,10},{9,11},{10,... | collective-permute-start | bytes 1572872 | tf_op jit(solution)/shard_map/ppermute | solution.py:327
  73.9 20.5 %collective-permute-start.6 = (bf16[512,512]{1,0:T(8,128)(2,1)}, bf16[512,512]{1,0:T(8,128)(2,1)}, u32[]{:S(2)}, u32[]{:S(2)}) collective-permute-start(bf16[512,512]{1,0:T(8,128)(2,1)} %collective-permute-done.5.refs_2_), channel_id=1, source_target_pairs={{0,4},{4,0},{8,12},{12,8},{16,20},{20,16},{24,28},{28,24},{1,5},{5... | collective-permute-start | bytes 1572872 | tf_op jit(solution)/shard_map/ppermute | solution.py:327
  75.0 22.1 %collective-permute-start.3 = (bf16[512,512]{1,0:T(8,128)(2,1)}, bf16[512,512]{1,0:T(8,128)(2,1)}, u32[]{:S(2)}, u32[]{:S(2)}) collective-permute-start(bf16[512,512]{1,0:T(8,128)(2,1)} %copy-done.18), channel_id=1, source_target_pairs={{0,4},{4,0},{8,12},{12,8},{16,20},{20,16},{24,28},{28,24},{1,5},{5... | collective-permute-start | bytes 1572872 | tf_op jit(solution)/shard_map/ppermute | solution.py:327
  75.3 24.9 %collective-permute-start.1 = (bf16[512,512]{1,0:T(8,128)(2,1)}, bf16[512,512]{1,0:T(8,128)(2,1)S(1)}, u32[]{:S(2)}, u32[]{:S(2)}) collective-permute-start(bf16[512,512]{1,0:T(8,128)(2,1)} %collective-permute-done.refs_0_), channel_id=1, source_target_pairs={{0,4},{4,0},{8,12},{12,8},{16,20},{20,16},{24,28},{28,24},{1,5},{5... | collective-permute-start | bytes 1572872 | tf_op jit(solution)/shard_map/ppermute | solution.py:327
  85.0 12.2 %copy-start.4 = (bf16[256,1024]{1,0:T(8,128)(2,1)S(1)}, bf16[256,1024]{1,0:T(8,128)(2,1)}, u32[]{:S(2)}) copy-start(bf16[256,1024]{1,0:T(8,128)(2,1)} %get-tuple-element.22.refs_5_.refs_8_.refs_10_) | copy-start | bytes 1572868
  85.1 16.4 %collective-permute-start.21 = (bf16[256,512]{1,0:T(8,128)(2,1)S(1)}, bf16[256,512]{1,0:T(8,128)(2,1)S(1)}, u32[]{:S(2)}, u32[]{:S(2)}) collective-permute-start(bf16[256,512]{1,0:T(8,128)(2,1)S(1)} %shard_map.51), channel_id=1, source_target_pairs={{0,1},{1,0},{2,3},{3,2},{4,5},{5,4},{6,7},{7,6},{8,9},{9,8},{10,11... | collective-permute-start | bytes 786440 | tf_op jit(solution)/shard_map/ppermute | solution.py:327
  94.3 12.8 %collective-permute-start.19 = (bf16[256,512]{1,0:T(8,128)(2,1)S(1)}, bf16[256,512]{1,0:T(8,128)(2,1)S(1)}, u32[]{:S(2)}, u32[]{:S(2)}) collective-permute-start(bf16[256,512]{1,0:T(8,128)(2,1)S(1)} %get-tuple-element.29), channel_id=1, source_target_pairs={{0,1},{1,0},{2,3},{3,2},{4,5},{5,4},{6,7},{7,6},{8,9},{9,8},{10,11... | collective-permute-start | bytes 786440 | tf_op jit(solution)/shard_map/ppermute | solution.py:327
  94.4 18.3 %collective-permute-start.20 = (bf16[256,512]{1,0:T(8,128)(2,1)S(1)}, bf16[256,512]{1,0:T(8,128)(2,1)S(1)}, u32[]{:S(2)}, u32[]{:S(2)}) collective-permute-start(bf16[256,512]{1,0:T(8,128)(2,1)S(1)} %shard_map.50), channel_id=1, source_target_pairs={{0,1},{1,0},{2,3},{3,2},{4,5},{5,4},{6,7},{7,6},{8,9},{9,8},{10,11... | collective-permute-start | bytes 786440 | tf_op jit(solution)/shard_map/ppermute | solution.py:327
  97.1 15.7 %copy-start.19 = (bf16[512,512]{1,0:T(8,128)(2,1)S(1)}, bf16[512,512]{1,0:T(8,128)(2,1)}, u32[]{:S(2)}) copy-start(bf16[512,512]{1,0:T(8,128)(2,1)} %copy-done.18) | copy-start | bytes 1572868
  97.1 20.8 %collective-permute-start.22 = (bf16[256,512]{1,0:T(8,128)(2,1)S(1)}, bf16[256,512]{1,0:T(8,128)(2,1)S(1)}, u32[]{:S(2)}, u32[]{:S(2)}) collective-permute-start(bf16[256,512]{1,0:T(8,128)(2,1)S(1)} %shard_map.53), channel_id=1, source_target_pairs={{0,1},{1,0},{2,3},{3,2},{4,5},{5,4},{6,7},{7,6},{8,9},{9,8},{10,11... | collective-permute-start | bytes 786440 | tf_op jit(solution)/shard_map/ppermute | solution.py:327
  119.1 4.6 %collective-permute-start.25 = (f32[8,128]{1,0:T(8,128)S(1)}, f32[8,128]{1,0:T(8,128)S(1)}, u32[]{:S(2)}, u32[]{:S(2)}) collective-permute-start(f32[8,128]{1,0:T(8,128)S(1)} %get-tuple-element.34.refs_0_), channel_id=1, source_target_pairs={{0,3},{1,2},{2,1},{3,0},{4,7},{5,6},{6,5},{7,4},{8,11},{9,10},{10,... | collective-permute-start | bytes 12296 | tf_op jit(solution)/shard_map/ppermute | solution.py:327
  120.6 3.6 %collective-permute-start.24 = (f32[8,128]{1,0:T(8,128)S(1)}, f32[8,128]{1,0:T(8,128)S(1)}, u32[]{:S(2)}, u32[]{:S(2)}) collective-permute-start(f32[8,128]{1,0:T(8,128)S(1)} %get-tuple-element.34.refs_0_), channel_id=1, source_target_pairs={{0,2},{1,3},{2,0},{3,1},{4,6},{5,7},{6,4},{7,5},{8,10},{9,11},{10,... | collective-permute-start | bytes 12296 | tf_op jit(solution)/shard_map/ppermute | solution.py:327
  122.3 3.6 %collective-permute-start.23 = (f32[8,128]{1,0:T(8,128)S(1)}, f32[8,128]{1,0:T(8,128)S(1)}, u32[]{:S(2)}, u32[]{:S(2)}) collective-permute-start(f32[8,128]{1,0:T(8,128)S(1)} %get-tuple-element.34.refs_0_), channel_id=1, source_target_pairs={{0,1},{1,0},{2,3},{3,2},{4,5},{5,4},{6,7},{7,6},{8,9},{9,8},{10,11... | collective-permute-start | bytes 12296 | tf_op jit(solution)/shard_map/ppermute | solution.py:327
  (14 other events, 25.7 us)
